TPU v7x, 32 devices: a whole 2x2x4 slice. The times are simulated.
32 devices in a mesh: batch: 2 (over x), seq: 16 (over z, y, core).
Axes of the slice: x: 2, y: 2, z: 4, core: 2. Of those that a mesh axis runs over, the one named last changes fastest.
Arguments:
- layer_input: bfloat16 [4, 2048, 768], P('batch', 'seq'), may hold values from -10 to 10
- query_weight: bfloat16 [768, 768], P(('batch', 'seq')), may hold values from -0.21875 to 0.21875
- key_weight: bfloat16 [768, 768], P(('batch', 'seq')), may hold values from -0.21875 to 0.21875
- value_weight: bfloat16 [768, 768], P(('batch', 'seq')), may hold values from -0.21875 to 0.21875
- output_weight: bfloat16 [768, 768], P(('batch', 'seq')), may hold values from -0.21875 to 0.21875
- up_weight: bfloat16 [768, 3072], P(('batch', 'seq')), may hold values from -0.21875 to 0.21875
- down_weight: bfloat16 [3072, 768], P(('batch', 'seq')), may hold values from -0.109375 to 0.109375
- query_bias: bfloat16 [768], P(('batch', 'seq')), may hold values from -3 to 3
- value_bias: bfloat16 [768], P(('batch', 'seq')), may hold values from -3 to 3
- output_bias: bfloat16 [768], P(('batch', 'seq')), may hold values from -3 to 3
- up_bias: bfloat16 [3072], P(('batch', 'seq')), may hold values from -3 to 3
- down_bias: bfloat16 [768], P(('batch', 'seq')), may hold values from -3 to 3
- first_gain: bfloat16 [768], P(('batch', 'seq')), may hold values from 0.25 to 1.75
- first_shift: bfloat16 [768], P(('batch', 'seq')), may hold values from -2 to 2
- second_gain: bfloat16 [768], P(('batch', 'seq')), may hold values from 0.25 to 1.75
- second_shift: bfloat16 [768], P(('batch', 'seq')), may hold values from -2 to 2
- mixing_taps: bfloat16 [12, 33], replicated, may hold values from -1 to 1
- output_cotangent: bfloat16 [4, 2048, 768], P('batch', 'seq'), may hold values from -6 to 6
Outputs:
- layer_output: bfloat16 [4, 2048, 768], P('batch', 'seq')
- input_gradient: float32 [4, 2048, 768], P('batch', 'seq')
- query_weight_gradient: float32 [768, 768], P(('batch', 'seq'))
- key_weight_gradient: float32 [768, 768], P(('batch', 'seq'))
- value_weight_gradient: float32 [768, 768], P(('batch', 'seq'))
- output_weight_gradient: float32 [768, 768], P(('batch', 'seq'))
- up_weight_gradient: float32 [768, 3072], P(('batch', 'seq'))
- down_weight_gradient: float32 [3072, 768], P(('batch', 'seq'))
- query_bias_gradient: float32 [768], P(('batch', 'seq'))
- value_bias_gradient: float32 [768], P(('batch', 'seq'))
- output_bias_gradient: float32 [768], P(('batch', 'seq'))
- up_bias_gradient: float32 [3072], P(('batch', 'seq'))
- down_bias_gradient: float32 [768], P(('batch', 'seq'))
- first_gain_gradient: float32 [768], P(('batch', 'seq'))
- first_shift_gradient: float32 [768], P(('batch', 'seq'))
- second_gain_gradient: float32 [768], P(('batch', 'seq'))
- second_shift_gradient: float32 [768], P(('batch', 'seq'))
- mixing_taps_gradient: float32 [12, 33], replicated
- pinv_error: float32 [], replicated
All inputs are finite; a program needn't handle non-finite values.
Results may differ from a plain program's by a relative error of at most 0.022.
The roundings to bfloat16 on the way count: a program that leaves them out, or rounds other values in their place, can miss the bound.
Values may be sent and summed in bfloat16 or wider, within the bound.
A program may use at most 192 MiB of HBM per device.

v0:
```python
from functools import partial

import jax
import jax.numpy as jnp
from jax import lax
from jax.experimental import pallas as pl
from jax.experimental.pallas import tpu as pltpu
from jax.sharding import PartitionSpec as P

MESH = pl.DeviceIdType.MESH
BATCH, SEQ = "batch", "seq"
BOTH = (BATCH, SEQ)
ROWS, SPREAD, TOKENS = P(BOTH, None), P(BOTH), P(BATCH, SEQ, None)
GATHER, SCATTER, NEXT, LAST = range(4)
ALL = slice(None)
LAG = 1


def grid_of(batch, seq):
    mid = 2 if seq < 32 else 4
    return batch, seq // (2 * mid), mid, 2


class Grid:
    def __init__(self, batch, seq):
        self.sizes = dict(zip("xzyc", grid_of(batch, seq)))
        s = lax.axis_index(SEQ)
        ny, nc = self.sizes["y"], self.sizes["c"]
        self.at = {"x": lax.axis_index(BATCH), "z": s // (ny * nc), "y": (s // nc) % ny, "c": s % nc}

    def device(self, at):
        return (at["x"], (at["z"] * self.sizes["y"] + at["y"]) * self.sizes["c"] + at["c"])

    def others(self, axis):
        size = self.sizes[axis]
        return [(step, lax.rem(self.at[axis] + step, size)) for step in range(1, size)]

    def moved(self, axis, other):
        return self.device({**self.at, axis: other})

    def greet(self):
        barrier = pltpu.get_barrier_semaphore()
        count = 0
        for axis in "zxyc":
            for _, other in self.others(axis):
                pl.semaphore_signal(barrier, inc=1, device_id=self.moved(axis, other), device_id_type=MESH)
                count += 1
        pl.semaphore_wait(barrier, count)

    def block(self, whole):
        return tuple(ALL if axis in whole else self.at[axis] for axis in "xzyc")


def gather_kernel(batch, seq, parts, orders, unit, n_in, *refs):
    ins, outs = refs[:n_in], refs[n_in : 2 * n_in]
    send_sem, recv_sem, own_sem = refs[2 * n_in :]
    g = Grid(batch, seq)
    g.greet()
    count = len(parts)
    copies = {}

    def view(part, whole):
        index, rows, cols = parts[part]
        return outs[index].at[g.block(whole) + (rows, cols)]

    def send(part, stage, axis, source, target):
        started = []
        for step, other in g.others(axis):
            copy = pltpu.make_async_remote_copy(
                src_ref=source,
                dst_ref=target,
                send_sem=send_sem.at[part, stage, step - 1],
                recv_sem=recv_sem.at[part, stage, step - 1],
                device_id=g.moved(axis, other),
                device_id_type=MESH,
            )
            copy.start()
            started.append(copy)
        copies[part, stage] = started

    def arrive(part, stage):
        for copy in copies[part, stage]:
            copy.wait_recv()

    def begin(part):
        index, rows, cols = parts[part]
        source = ins[index].at[rows, cols]
        own = pltpu.make_async_copy(source, view(part, ""), own_sem.at[part])
        own.start()
        copies[part, "own"] = own
        send(part, 0, "z", source, view(part, ""))

    def spread(stage):
        def run(part):
            axes = ("z",) + tuple(orders[part]) + ("c",)
            if stage == 1:
                copies[part, "own"].wait()
            arrive(part, stage - 1)
            if stage < 4:
                held = view(part, axes[:stage])
                send(part, stage, axes[stage], held, held)
        return run

    units = [range(at, min(at + unit, count)) for at in range(0, count, unit)]
    stages = [begin] + [spread(stage) for stage in (1, 2, 3, 4)]
    for turn in range(len(units) + 4 * LAG):
        for lag, stage in enumerate(stages):
            if 0 <= turn - lag * LAG < len(units):
                for part in units[turn - lag * LAG]:
                    stage(part)
    for part in range(count):
        for stage in range(4):
            for copy in copies[part, stage]:
                copy.wait_send()


def gather_weights(batch, seq, shards, parts, orders, unit, collective_id):
    sizes = grid_of(batch, seq)
    n, count, most = len(shards), len(parts), max(sizes) - 1
    return pl.pallas_call(
        partial(gather_kernel, batch, seq, parts, orders, unit, n),
        out_shape=[jax.ShapeDtypeStruct(sizes + s.shape, s.dtype) for s in shards],
        in_specs=[pl.BlockSpec(memory_space=pltpu.VMEM)] * n,
        out_specs=[pl.BlockSpec(memory_space=pl.ANY)] * n,
        scratch_shapes=[
            pltpu.SemaphoreType.DMA((count, 4, most)),
            pltpu.SemaphoreType.DMA((count, 4, most)),
            pltpu.SemaphoreType.DMA((count,)),
        ],
        compiler_params=pltpu.CompilerParams(collective_id=collective_id, has_side_effects=True),
        name="gather_weights",
    )(*shards)


def scatter_kernel(batch, seq, parts, orders, unit, n_in, *refs):
    ins, outs = refs[:n_in], refs[n_in : 2 * n_in]
    own_sem, send_sem, recv_sem = refs[-3:]
    scratch = refs[2 * n_in : -3]
    g = Grid(batch, seq)
    g.greet()
    count = len(parts)
    copies = {}
    shapes = [part_shape(ins, part) for part in parts]
    groups = sorted(set(shapes), key=shapes.index)
    held, from_core, far, from_near, from_line = ([None] * count for _ in range(5))
    for at, shape in enumerate(groups):
        members = [part for part in range(count) if shapes[part] == shape]
        buffers = scratch[6 * at : 6 * at + 6]
        for rank, part in enumerate(members):
            far_rank = [p for p in members if orders[p] == orders[part]].index(part)
            held[part], from_core[part] = buffers[0].at[rank], buffers[1].at[rank]
            far[part] = (buffers[2] if orders[part][1] == "y" else buffers[3]).at[far_rank]
            from_near[part], from_line[part] = buffers[4].at[rank], buffers[5].at[rank]

    def source(part, core):
        index, rows, cols = parts[part]
        return ins[index].at[ALL, ALL, ALL, core, rows, cols]

    def mine(part, whole, **moved):
        at = {**g.at, **moved}
        return held[part].at[tuple(ALL if axis in whole else at[axis] for axis in "xzy")]

    def send(part, stage, axis, step, other, src, dst):
        copy = pltpu.make_async_remote_copy(
            src_ref=src,
            dst_ref=dst,
            send_sem=send_sem.at[part, stage, step - 1],
            recv_sem=recv_sem.at[part, stage, step - 1],
            device_id=g.moved(axis, other),
            device_id_type=MESH,
        )
        copy.start()
        copies.setdefault((part, stage), []).append(copy)

    def accumulate(into, others):
        lead = into.shape[:-2]
        total = 1
        for size in lead:
            total *= size

        def step(i, carry):
            at = []
            for size in reversed(lead):
                at.insert(0, i % size)
                i = i // size
            at = tuple(at)
            value = into[at].astype(jnp.float32)
            for other in others:
                value += other[at].astype(jnp.float32)
            into[at] = value.astype(into.dtype)
            return carry

        lax.fori_loop(0, total, step, 0)

    def begin(part):
        own = pltpu.make_async_copy(source(part, g.at["c"]), held[part], own_sem.at[part])
        own.start()
        copies[part, "own"] = own
        for step, other in g.others("c"):
            send(part, 0, "c", step, other, source(part, other), from_core[part])

    def arrive(part, stage):
        for copy in copies[part, stage]:
            copy.wait_recv()

    def reduce_core(part):
        copies[part, "own"].wait()
        arrive(part, 0)
        accumulate(held[part], [from_core[part]])
        axis = orders[part][1]
        whole = "xzy".replace(axis, "")
        for step, other in g.others(axis):
            send(part, 1, axis, step, other, mine(part, whole, **{axis: other}), far[part].at[step - 1])

    def reduce_far(part):
        arrive(part, 1)
        near, axis = orders[part]
        accumulate(
            mine(part, "xzy".replace(axis, "")), [far[part].at[step - 1] for step, _ in g.others(axis)]
        )
        for step, other in g.others(near):
            send(part, 2, near, step, other, mine(part, "z", **{near: other}), from_near[part].at[step - 1])

    def reduce_near(part):
        arrive(part, 2)
        near = orders[part][0]
        accumulate(mine(part, "z"), [from_near[part].at[step - 1] for step, _ in g.others(near)])
        for step, other in g.others("z"):
            send(part, 3, "z", step, other, mine(part, "", z=other), from_line[part].at[step - 1])

    def reduce_line(part):
        arrive(part, 3)
        index, rows, cols = parts[part]
        value = mine(part, "")[...].astype(jnp.float32)
        for step, _ in g.others("z"):
            value += from_line[part][step - 1].astype(jnp.float32)
        outs[index][rows, cols] = value

    units = [range(at, min(at + unit, count)) for at in range(0, count, unit)]
    stages = [begin, reduce_core, reduce_far, reduce_near, reduce_line]
    for turn in range(len(units) + 4 * LAG):
        for lag, stage in enumerate(stages):
            if 0 <= turn - lag * LAG < len(units):
                for part in units[turn - lag * LAG]:
                    stage(part)
    for part in range(count):
        for stage in range(4):
            for copy in copies[part, stage]:
                copy.wait_send()


def part_shape(arrays, part):
    index, rows, cols = part
    array = arrays[index]
    spans = [len(range(*span.indices(size))) for span, size in zip((rows, cols), array.shape[-2:])]
    return (*spans, array.dtype)


def scatter_grads(batch, seq, grads, parts, orders, unit, collective_id):
    sizes = nx, nz, ny, nc = grid_of(batch, seq)
    n, count, most = len(grads), len(parts), max(sizes) - 1
    shapes = [part_shape(grads, part) for part in parts]
    scratch = []
    for shape in sorted(set(shapes), key=shapes.index):
        members = [part for part in range(count) if shapes[part] == shape]
        rows, cols, kind = shape
        ways = [orders[part] for part in members]
        total = len(members)
        scratch += [
            pltpu.VMEM((total, nx, nz, ny, rows, cols), kind),
            pltpu.VMEM((total, nx, nz, ny, rows, cols), kind),
            pltpu.VMEM((max(1, ways.count("xy")), ny - 1, nx, nz, rows, cols), kind),
            pltpu.VMEM((max(1, ways.count("yx")), nx - 1, nz, ny, rows, cols), kind),
            pltpu.VMEM((total, max(nx, ny) - 1, nz, rows, cols), kind),
            pltpu.VMEM((total, nz - 1, rows, cols), kind),
        ]
    return pl.pallas_call(
        partial(scatter_kernel, batch, seq, parts, orders, unit, n),
        out_shape=[jax.ShapeDtypeStruct(s.shape[4:], jnp.float32) for s in grads],
        in_specs=[pl.BlockSpec(memory_space=pl.ANY)] * n,
        out_specs=[pl.BlockSpec(memory_space=pltpu.VMEM)] * n,
        scratch_shapes=scratch
        + [
            pltpu.SemaphoreType.DMA((count,)),
            pltpu.SemaphoreType.DMA((count, 4, most)),
            pltpu.SemaphoreType.DMA((count, 4, most)),
        ],
        compiler_params=pltpu.CompilerParams(
            collective_id=collective_id, has_side_effects=True, vmem_limit_bytes=48 * 2**20
        ),
        name="scatter_grads",
    )(*grads)


HEADS = 12
HEAD_DIM = 64
LANDMARKS = 64
KERNEL = 33
NEWTON = 6
RIM = 16
FEATURES = HEADS * HEAD_DIM


highest_precision = lax.Precision.HIGHEST


def with_halo(x, sides, width):
    for axis, dim in sides:
        size, length = (lax.axis_size(axis), x.shape[dim])
        up = [(i, (i + 1) % size) for i in range(size - 1)]
        down = [(j, i) for i, j in up]
        last = lax.slice_in_dim(x, length - width, length, axis=dim)
        initial = lax.slice_in_dim(x, 0, width, axis=dim)
        before = lax.ppermute(last, axis, up)
        after = lax.ppermute(initial, axis, down)
        x = jnp.concatenate([before, x, after], axis=dim)
    return x


def merged(value, axis, join):
    pieces = jax.tree.map(lambda part: lax.all_gather(part, axis), value)
    head = jax.tree.map(lambda part: part[0], pieces)
    tail = jax.tree.map(lambda part: part[1:], pieces)
    subtotal, _ = lax.scan(lambda subtotal, piece: (join(subtotal, piece), None), head, tail)
    return subtotal


def for_sending(x):
    return jax.tree.map(lambda a: a.astype(jnp.bfloat16) if a.dtype == jnp.float32 else a, x)


def shifted(block, axis, distance):
    devices = range(lax.axis_size(axis))
    route = [(i - distance, i) for i in devices if i - distance in devices]
    return lax.ppermute(block, axis, route)


def layer_norm(rows, gain, shift):
    centre = rows - jnp.mean(rows, axis=-1, keepdims=True)
    spread = jnp.mean(centre * centre, axis=-1, keepdims=True)
    return centre * lax.rsqrt(spread + 1e-05) * gain + shift


def split_heads(matrix):
    return matrix.reshape(matrix.shape[:-1] + (HEADS, HEAD_DIM))


def pseudo_inverse(landmark_kernel_matrix):
    column_top = jnp.max(jnp.sum(landmark_kernel_matrix, axis=-2), axis=-1)
    row_top = jnp.max(jnp.sum(landmark_kernel_matrix, axis=-1), axis=-1)
    approx = jnp.swapaxes(landmark_kernel_matrix, -1, -2) / (column_top * row_top)[..., None, None]
    ident = jnp.eye(landmark_kernel_matrix.shape[-1], dtype=jnp.float32)
    for turn_index in range(NEWTON):
        product = jnp.matmul(landmark_kernel_matrix, approx, precision=highest_precision)
        inner = 7.0 * ident - product
        inner = 15.0 * ident - jnp.matmul(product, inner, precision=highest_precision)
        inner = 13.0 * ident - jnp.matmul(product, inner, precision=highest_precision)
        approx = 0.25 * jnp.matmul(approx, inner, precision=highest_precision)
    return approx


def landmark_mix(mark_query, mark_key, distant_values):
    scale = HEAD_DIM ** (-0.25)
    scores = jnp.einsum(
        "smhd,snhd->shmn",
        split_heads(mark_query) * scale,
        split_heads(mark_key) * scale,
        precision=highest_precision,
    )
    landmark_kernel_matrix = jax.nn.softmax(scores, axis=-1)
    inverse = pseudo_inverse(landmark_kernel_matrix)
    mixing_result = jnp.matmul(inverse, distant_values, precision=highest_precision)
    ident = jnp.eye(landmark_kernel_matrix.shape[-1], dtype=jnp.float32)
    defect = ident - jnp.matmul(landmark_kernel_matrix, inverse, precision=highest_precision)
    error = jnp.sum(jnp.sqrt(jnp.sum(defect * defect, axis=(-2, -1))))
    return (mixing_result, error)


def near_mix(queries, mark_key, mixing_result, value_ext, taps):
    scale = HEAD_DIM ** (-0.25)
    scores = jnp.einsum(
        "sthd,smhd->shtm",
        split_heads(queries) * scale,
        split_heads(mark_key) * scale,
        precision=highest_precision,
    )
    nearby_part = jax.nn.softmax(scores, axis=-1)
    attended_output = jnp.einsum(
        "shtm,shmd->sthd", nearby_part, mixing_result, precision=highest_precision
    )
    window = split_heads(value_ext)
    length = queries.shape[1]
    for tap_index in range(KERNEL):
        attended_output = (
            attended_output
            + taps[:, tap_index][:, None] * window[:, tap_index : tap_index + length]
        )
    return attended_output.reshape(queries.shape)


def far_scores(mark_query, key_rows):
    scale = HEAD_DIM ** (-0.25)
    return jnp.einsum(
        "smhd,sthd->shmt",
        split_heads(mark_query) * scale,
        split_heads(key_rows) * scale,
        precision=highest_precision,
    )


def far_stats(mark_query, key_rows, value_rows):
    scores = far_scores(mark_query, key_rows)
    peak = jnp.max(scores, axis=-1)
    expo = jnp.exp(scores - peak[..., None])
    total = jnp.sum(expo, axis=-1)
    numer = jnp.einsum(
        "shmt,sthd->shmd", expo, split_heads(value_rows), precision=highest_precision
    )
    return (peak, total, numer)


def far_change(mark_query, key_rows, value_rows, peak, total, distant_values):
    expo = jnp.exp(far_scores(mark_query, key_rows) - peak[..., None])
    numer = jnp.einsum(
        "shmt,sthd->shmd", expo, split_heads(value_rows), precision=highest_precision
    )
    return (numer - distant_values * jnp.sum(expo, axis=-1)[..., None]) / total[..., None]


def combine_stats(first, second):
    peak = jnp.maximum(first[0], second[0])
    first_weight = jnp.exp(first[0] - peak)
    second_weight = jnp.exp(second[0] - peak)
    total = first[1] * first_weight + second[1] * second_weight
    numer = first[2] * first_weight[..., None] + second[2] * second_weight[..., None]
    return (peak, total, numer)


def big_product(left, right):
    return jnp.einsum("std,de->ste", left, right, preferred_element_type=jnp.float32)


def weight_grad(left, right):
    return jnp.einsum("std,ste->de", left, right, preferred_element_type=jnp.float32)


def back_product(delta, weight):
    return jnp.einsum("ste,de->std", delta, weight, preferred_element_type=jnp.float32)


def bias_sum(delta):
    return jnp.sum(delta.astype(jnp.float32), axis=(0, 1))


def comm_parts(rows, wide):
    width = FEATURES
    parts = [(at, ALL, ALL) for at in range(4)]
    parts += [(4, ALL, slice(at * width, (at + 1) * width)) for at in range(wide)]
    parts += [(5, slice(at * rows, (at + 1) * rows), ALL) for at in range(wide)]
    return parts + [(6, ALL, ALL)]


def local(
    layer_input,
    query_weight,
    key_weight,
    value_weight,
    output_weight,
    up_weight,
    down_weight,
    query_bias,
    value_bias,
    output_bias,
    up_bias,
    down_bias,
    first_gain,
    first_shift,
    second_gain,
    second_shift,
    mixing_taps,
    output_cotangent,
):
    (
        full_query,
        full_key,
        full_value,
        full_output,
        full_up,
        full_down,
        bias_query,
        bias_value,
        bias_output,
        bias_up,
        bias_down,
        gain_first,
        shift_first,
        gain_second,
        shift_second,
    ) = (
        lax.all_gather(query_weight, BOTH, axis=0, tiled=True),
        lax.all_gather(key_weight, BOTH, axis=0, tiled=True),
        lax.all_gather(value_weight, BOTH, axis=0, tiled=True),
        lax.all_gather(output_weight, BOTH, axis=0, tiled=True),
        lax.all_gather(up_weight, BOTH, axis=0, tiled=True),
        lax.all_gather(down_weight, BOTH, axis=0, tiled=True),
        lax.all_gather(query_bias, BOTH, axis=0, tiled=True),
        lax.all_gather(value_bias, BOTH, axis=0, tiled=True),
        lax.all_gather(output_bias, BOTH, axis=0, tiled=True),
        lax.all_gather(up_bias, BOTH, axis=0, tiled=True),
        lax.all_gather(down_bias, BOTH, axis=0, tiled=True),
        lax.all_gather(first_gain, BOTH, axis=0, tiled=True),
        lax.all_gather(first_shift, BOTH, axis=0, tiled=True),
        lax.all_gather(second_gain, BOTH, axis=0, tiled=True),
        lax.all_gather(second_shift, BOTH, axis=0, tiled=True),
    )
    local_marks = LANDMARKS // lax.axis_size(SEQ)
    batch_rows, tokens, features = layer_input.shape
    segment = tokens // local_marks
    queries = big_product(layer_input, full_query) + bias_query.astype(jnp.float32)
    key_rows = big_product(layer_input, full_key)
    value_rows = (big_product(layer_input, full_value) + bias_value.astype(jnp.float32)).astype(
        jnp.bfloat16
    )
    mark_query = jnp.mean(
        queries.reshape(batch_rows, local_marks, segment, features), axis=2
    ).astype(jnp.bfloat16)
    mark_key = jnp.mean(
        key_rows.reshape(batch_rows, local_marks, segment, features), axis=2
    ).astype(jnp.bfloat16)
    all_query, all_key = (
        lax.all_gather(mark_query, SEQ, axis=1, tiled=True),
        lax.all_gather(mark_key, SEQ, axis=1, tiled=True),
    )
    value_ext = with_halo(value_rows, ((SEQ, 1),), RIM)
    query_marks = all_query.astype(jnp.float32)
    key_marks = all_key.astype(jnp.float32)
    value_float = value_rows.astype(jnp.float32)
    ext_float = value_ext.astype(jnp.float32)
    taps = mixing_taps.astype(jnp.float32)
    stat_peak, stat_total, stat_numer = far_stats(query_marks, key_rows, value_float)
    peak, total, numer = merged((stat_peak, stat_total, stat_numer), SEQ, combine_stats)
    distant_values = numer / total[..., None]
    mixing_result, mix_back, error = jax.vjp(
        landmark_mix, query_marks, key_marks, distant_values, has_aux=True
    )
    attended_output, near_back = jax.vjp(
        near_mix, queries, key_marks, mixing_result, ext_float, taps
    )
    attention = attended_output.astype(jnp.bfloat16)
    resid_first = (
        layer_input.astype(jnp.float32)
        + big_product(attention, full_output)
        + bias_output.astype(jnp.float32)
    )
    hidden, first_back = jax.vjp(
        layer_norm, resid_first, gain_first.astype(jnp.float32), shift_first.astype(jnp.float32)
    )
    hidden_low = hidden.astype(jnp.bfloat16)
    upper = big_product(hidden_low, full_up) + bias_up.astype(jnp.float32)
    activated, gelu_back = jax.vjp(partial(jax.nn.gelu, approximate=False), upper)
    activated_low = activated.astype(jnp.bfloat16)
    resid_second = hidden + big_product(activated_low, full_down) + bias_down.astype(jnp.float32)
    normed, second_back = jax.vjp(
        layer_norm, resid_second, gain_second.astype(jnp.float32), shift_second.astype(jnp.float32)
    )
    layer_output = normed.astype(jnp.bfloat16)
    pinv_error = lax.psum(error, BATCH) / (batch_rows * lax.axis_size(BATCH) * HEADS)
    delta_second, second_gain_grad, second_shift_grad = second_back(
        output_cotangent.astype(jnp.float32)
    )
    delta_lower = delta_second.astype(jnp.bfloat16)
    down_grad = weight_grad(activated_low, delta_lower)
    down_bias_grad = bias_sum(delta_lower)
    delta_upper = gelu_back(back_product(delta_lower, full_down))[0].astype(jnp.bfloat16)
    up_grad = weight_grad(hidden_low, delta_upper)
    up_bias_grad = bias_sum(delta_upper)
    delta_hidden = back_product(delta_upper, full_up) + delta_second
    delta_first, first_gain_grad, first_shift_grad = first_back(delta_hidden)
    delta_proj = delta_first.astype(jnp.bfloat16)
    output_grad = weight_grad(attention, delta_proj)
    output_bias_grad = bias_sum(delta_proj)
    delta_attention = back_product(delta_proj, full_output)
    delta_queries, key_part, mixing_part, delta_ext, taps_part = near_back(delta_attention)
    delta_mixing = jax.tree.map(
        lambda part: part.astype(jnp.float32), lax.psum(for_sending(mixing_part), SEQ)
    )
    query_rep, key_rep, delta_far = mix_back(delta_mixing)
    far_back = jax.vjp(
        partial(far_change, peak=peak, total=total, distant_values=distant_values),
        query_marks,
        key_rows,
        value_float,
    )[1]
    far_query, far_keys, far_vals = far_back(delta_far)
    own_key, own_query = (
        lax.psum_scatter(
            key_part.astype(jnp.bfloat16), SEQ, scatter_dimension=1, tiled=True
        ).astype(jnp.float32),
        lax.psum_scatter(
            far_query.astype(jnp.bfloat16), SEQ, scatter_dimension=1, tiled=True
        ).astype(jnp.float32),
    )
    start = lax.axis_index(SEQ) * local_marks
    own_query = own_query + lax.dynamic_slice_in_dim(query_rep, start, local_marks, 1)
    own_key = own_key + lax.dynamic_slice_in_dim(key_rep, start, local_marks, 1)

    def spread_marks(marks):
        shaped = jnp.broadcast_to(
            (marks / segment)[:, :, None, :], (batch_rows, local_marks, segment, features)
        )
        return shaped.reshape(batch_rows, tokens, features)

    query_delta = (delta_queries + spread_marks(own_query)).astype(jnp.bfloat16)
    key_delta = (far_keys + spread_marks(own_key)).astype(jnp.bfloat16)
    from_left = shifted(for_sending(delta_ext[:, :RIM]), SEQ, -1)
    from_right = shifted(for_sending(delta_ext[:, tokens + RIM :]), SEQ, 1)
    value_sum = delta_ext[:, RIM : RIM + tokens] + far_vals
    value_sum = value_sum + jnp.pad(from_left, ((0, 0), (tokens - RIM, 0), (0, 0)))
    value_sum = value_sum + jnp.pad(from_right, ((0, 0), (0, tokens - RIM), (0, 0)))
    value_delta = value_sum.astype(jnp.bfloat16)
    query_grad = weight_grad(layer_input, query_delta)
    key_grad = weight_grad(layer_input, key_delta)
    value_grad = weight_grad(layer_input, value_delta)
    query_bias_grad = bias_sum(query_delta)
    value_bias_grad = bias_sum(value_delta)
    input_gradient = (
        back_product(query_delta, full_query)
        + back_product(key_delta, full_key)
        + back_product(value_delta, full_value)
        + delta_first
    )
    taps_gradient = lax.psum(taps_part, BOTH)
    owned = (
        lax.psum_scatter(query_grad, BOTH, scatter_dimension=0, tiled=True),
        lax.psum_scatter(key_grad, BOTH, scatter_dimension=0, tiled=True),
        lax.psum_scatter(value_grad, BOTH, scatter_dimension=0, tiled=True),
        lax.psum_scatter(output_grad, BOTH, scatter_dimension=0, tiled=True),
        lax.psum_scatter(up_grad, BOTH, scatter_dimension=0, tiled=True),
        lax.psum_scatter(down_grad, BOTH, scatter_dimension=0, tiled=True),
        lax.psum_scatter(query_bias_grad, BOTH, scatter_dimension=0, tiled=True),
        lax.psum_scatter(value_bias_grad, BOTH, scatter_dimension=0, tiled=True),
        lax.psum_scatter(output_bias_grad, BOTH, scatter_dimension=0, tiled=True),
        lax.psum_scatter(up_bias_grad, BOTH, scatter_dimension=0, tiled=True),
        lax.psum_scatter(down_bias_grad, BOTH, scatter_dimension=0, tiled=True),
        lax.psum_scatter(first_gain_grad, BOTH, scatter_dimension=0, tiled=True),
        lax.psum_scatter(first_shift_grad, BOTH, scatter_dimension=0, tiled=True),
        lax.psum_scatter(second_gain_grad, BOTH, scatter_dimension=0, tiled=True),
        lax.psum_scatter(second_shift_grad, BOTH, scatter_dimension=0, tiled=True),
    )
    return (
        layer_output,
        input_gradient,
        owned[0],
        owned[1],
        owned[2],
        owned[3],
        owned[4],
        owned[5],
        owned[6],
        owned[7],
        owned[8],
        owned[9],
        owned[10],
        owned[11],
        owned[12],
        owned[13],
        owned[14],
        taps_gradient,
        pinv_error,
    )


def exchange_kernel(ways, *refs):
    n = len(ways)
    ins, outs = refs[:n], refs[n : 2 * n]
    send_sem, recv_sem = refs[2 * n :]
    size = lax.axis_size(SEQ)
    batch, me = lax.axis_index(BATCH), lax.axis_index(SEQ)
    barrier = pltpu.get_barrier_semaphore()

    def greet(step, carry):
        peer = lax.rem(me + step, size)
        pl.semaphore_signal(barrier, inc=1, device_id=(batch, peer), device_id_type=MESH)
        return carry

    lax.fori_loop(1, size, greet, 0)
    pl.semaphore_wait(barrier, size - 1)

    def copy_of(at, step):
        peer = lax.rem(me + step, size)
        source = ins[at].at[peer] if ways[at] == SCATTER else ins[at]
        target = outs[at].at[me] if ways[at] in (GATHER, SCATTER) else outs[at]
        return pltpu.make_async_remote_copy(
            src_ref=source,
            dst_ref=target,
            send_sem=send_sem.at[at, step],
            recv_sem=recv_sem.at[at, step],
            device_id=(batch, peer),
            device_id_type=MESH,
        )

    def start(step, carry):
        for at, way in enumerate(ways):
            if way in (GATHER, SCATTER):
                copy_of(at, step).start()
        return carry

    def finish(step, carry):
        for at, way in enumerate(ways):
            if way in (GATHER, SCATTER):
                copy_of(at, step).wait()
        return carry

    single = [(at, {NEXT: 1, LAST: size - 1}[way]) for at, way in enumerate(ways) if way in (NEXT, LAST)]
    for at, step in single:
        copy_of(at, step).start()
    lax.fori_loop(1, size, start, 0)
    for at, way in enumerate(ways):
        if way == GATHER:
            outs[at][me] = ins[at][...]
        elif way == SCATTER:
            outs[at][me] = ins[at][me]
    for at, step in single:
        copy_of(at, step).wait()
    lax.fori_loop(1, size, finish, 0)


def exchange(size, collective_id, *items):
    ways = tuple(way for way, _ in items)
    arrays = [array for _, array in items]
    shapes = [((size,) + a.shape if way == GATHER else a.shape) for way, a in items]
    vmem = pl.BlockSpec(memory_space=pltpu.VMEM)
    return pl.pallas_call(
        partial(exchange_kernel, ways),
        out_shape=[jax.ShapeDtypeStruct(shape, a.dtype) for shape, a in zip(shapes, arrays)],
        in_specs=[vmem] * len(ways),
        out_specs=[vmem] * len(ways),
        scratch_shapes=[
            pltpu.SemaphoreType.DMA((len(ways), size)),
            pltpu.SemaphoreType.DMA((len(ways), size)),
        ],
        compiler_params=pltpu.CompilerParams(collective_id=collective_id, has_side_effects=True),
        name="exchange",
    )(*arrays)


def own_mix(mark_query, mark_key, distant_values):
    scale = HEAD_DIM ** (-0.25)
    heads = distant_values.shape[0]

    def pair(marks):
        return marks.reshape(marks.shape[0], heads, HEAD_DIM) * scale

    scores = jnp.einsum("mhd,nhd->hmn", pair(mark_query), pair(mark_key), precision=highest_precision)
    landmark_kernel_matrix = jax.nn.softmax(scores, axis=-1)
    inverse = pseudo_inverse(landmark_kernel_matrix)
    mixing_result = jnp.matmul(inverse, distant_values, precision=highest_precision)
    ident = jnp.eye(landmark_kernel_matrix.shape[-1], dtype=jnp.float32)
    defect = ident - jnp.matmul(landmark_kernel_matrix, inverse, precision=highest_precision)
    error = jnp.sum(jnp.sqrt(jnp.sum(defect * defect, axis=(-2, -1))))
    return (mixing_result, error)


def far_back(mark_query, key_rows, value_rows, peak, total, delta_far, inner):
    scale = HEAD_DIM ** (-0.25)
    near_one = jnp.exp(far_scores(mark_query, key_rows) - peak[..., None]) / total[..., None]
    values = split_heads(value_rows)
    far_vals = jnp.einsum("shmt,shmd->sthd", near_one, delta_far, precision=highest_precision)
    slope = jnp.einsum("shmd,sthd->shmt", delta_far, values, precision=highest_precision)
    slope = near_one * (slope - inner[..., None])
    far_query = jnp.einsum("shmt,sthd->smhd", slope, split_heads(key_rows) * scale, precision=highest_precision)
    far_keys = jnp.einsum("shmt,smhd->sthd", slope, split_heads(mark_query) * scale, precision=highest_precision)
    return (
        (far_query * scale).reshape(mark_query.shape),
        (far_keys * scale).reshape(key_rows.shape),
        far_vals.reshape(value_rows.shape),
    )


def local_fast(
    batch,
    seq,
    layer_input,
    query_weight,
    key_weight,
    value_weight,
    output_weight,
    up_weight,
    down_weight,
    query_bias,
    value_bias,
    output_bias,
    up_bias,
    down_bias,
    first_gain,
    first_shift,
    second_gain,
    second_shift,
    mixing_taps,
    output_cotangent,
):
    weights = (query_weight, key_weight, value_weight, output_weight, up_weight, down_weight)
    vectors = (
        query_bias,
        value_bias,
        output_bias,
        down_bias,
        first_gain,
        first_shift,
        second_gain,
        second_shift,
    )
    own = query_bias.shape[0]
    wide = up_bias.shape[0] // own
    packed = jnp.concatenate([*(v[None] for v in vectors), up_bias.reshape(wide, own)], axis=0)
    packed = jnp.pad(packed, ((0, 16 - packed.shape[0]), (0, 128 - own)))
    parts = comm_parts(own, wide)
    orders = ["xy" if at % 2 == 0 else "yx" for at in range(len(parts))]
    *gathered, vectors_all = gather_weights(
        batch, seq, weights + (packed,), parts, orders, 2, 1
    )
    full_query, full_key, full_value, full_output, full_up, full_down = (
        whole.reshape(-1, whole.shape[-1]) for whole in gathered
    )
    table = jnp.swapaxes(vectors_all.reshape(batch * seq, 16, 128)[:, :, :own], 0, 1)
    (
        bias_query,
        bias_value,
        bias_output,
        bias_down,
        gain_first,
        shift_first,
        gain_second,
        shift_second,
    ) = (table[at].reshape(-1) for at in range(8))
    bias_up = jnp.swapaxes(table[8 : 8 + wide], 0, 1).reshape(-1)
    local_marks = LANDMARKS // lax.axis_size(SEQ)
    batch_rows, tokens, features = layer_input.shape
    segment = tokens // local_marks
    queries = big_product(layer_input, full_query) + bias_query.astype(jnp.float32)
    key_rows = big_product(layer_input, full_key)
    value_rows = (big_product(layer_input, full_value) + bias_value.astype(jnp.float32)).astype(
        jnp.bfloat16
    )
    mark_query = jnp.mean(
        queries.reshape(batch_rows, local_marks, segment, features), axis=2
    ).astype(jnp.bfloat16)
    mark_key = jnp.mean(
        key_rows.reshape(batch_rows, local_marks, segment, features), axis=2
    ).astype(jnp.bfloat16)
    marks, before, after = exchange(
        seq,
        3,
        (GATHER, jnp.stack([mark_query, mark_key])),
        (NEXT, value_rows[:, tokens - RIM :]),
        (LAST, value_rows[:, :RIM]),
    )
    place_at = lax.axis_index(SEQ)
    before = jnp.where(place_at > 0, before, jnp.zeros_like(before))
    after = jnp.where(place_at < seq - 1, after, jnp.zeros_like(after))
    value_ext = jnp.concatenate([before, value_rows, after], axis=1)
    marks = jnp.transpose(marks, (1, 2, 0, 3, 4)).reshape(2, batch_rows, LANDMARKS, features)
    query_marks, key_marks = marks[0].astype(jnp.float32), marks[1].astype(jnp.float32)
    value_float = value_rows.astype(jnp.float32)
    ext_float = value_ext.astype(jnp.float32)
    taps = mixing_taps.astype(jnp.float32)
    stat_peak, stat_total, stat_numer = far_stats(query_marks, key_rows, value_float)
    owners = batch_rows * HEADS // 2
    low = jnp.bfloat16

    def to_owners(matrices):
        pairs = matrices.reshape(owners, 2, LANDMARKS, HEAD_DIM).astype(low)
        pairs = jnp.swapaxes(pairs, 1, 2).reshape(owners, LANDMARKS, 2 * HEAD_DIM)
        return jnp.concatenate([pairs, pairs[: seq - owners]], axis=0)

    def as_pair(sides):
        return jnp.swapaxes(sides.reshape(LANDMARKS, 2, HEAD_DIM), 0, 1)

    def as_sides(pair):
        return jnp.swapaxes(pair, 0, 1).reshape(LANDMARKS, 2 * HEAD_DIM)

    def from_owners(sides):
        pairs = sides[:owners].reshape(owners, LANDMARKS, 2, HEAD_DIM).astype(jnp.float32)
        return jnp.swapaxes(pairs, 1, 2).reshape(batch_rows, HEADS, LANDMARKS, HEAD_DIM)

    def rows_to_owners(*rows):
        table = jnp.stack([row.reshape(owners, 2 * LANDMARKS) for row in rows], axis=1)
        table = jnp.pad(table, ((0, 0), (0, 8 - len(rows)), (0, 0)))
        return jnp.concatenate([table, table[: seq - owners]], axis=0)

    def rows_from_owners(table, at):
        return table[:owners, at].reshape(batch_rows, HEADS, LANDMARKS)

    numers, stats = exchange(
        seq,
        4,
        (SCATTER, to_owners(stat_numer)),
        (SCATTER, rows_to_owners(stat_peak, stat_total)),
    )
    peak_rows, total_rows = stats[:, 0], stats[:, 1]
    peak_own = jnp.max(peak_rows, axis=0)
    weights_own = jnp.exp(peak_rows - peak_own)
    total_own = jnp.sum(total_rows * weights_own, axis=0)
    numer_pairs = jnp.swapaxes(numers.astype(jnp.float32).reshape(seq, LANDMARKS, 2, HEAD_DIM), 1, 2)
    shares = (weights_own / total_own).reshape(seq, 2, LANDMARKS, 1)
    distant_own = jnp.sum(numer_pairs * shares, axis=0)
    owner = lax.rem(place_at, owners)
    own_row, own_lane = owner // (HEADS // 2), (owner % (HEADS // 2)) * 2 * HEAD_DIM

    def own_marks(all_marks):
        return lax.dynamic_slice(all_marks, (own_row, 0, own_lane), (1, LANDMARKS, 2 * HEAD_DIM))[0]

    mixing_own, mix_back, error = jax.vjp(
        own_mix, own_marks(query_marks), own_marks(key_marks), distant_own, has_aux=True
    )
    mixings, stats = exchange(
        seq,
        5,
        (GATHER, as_sides(mixing_own).astype(low)),
        (GATHER, jnp.pad(jnp.stack([peak_own, total_own]), ((0, 6), (0, 0)))),
    )
    mixing_result = from_owners(mixings)
    peak, total = rows_from_owners(stats, 0), rows_from_owners(stats, 1)
    attended_output, near_back = jax.vjp(
        near_mix, queries, key_marks, mixing_result, ext_float, taps
    )
    attention = attended_output.astype(jnp.bfloat16)
    resid_first = (
        layer_input.astype(jnp.float32)
        + big_product(attention, full_output)
        + bias_output.astype(jnp.float32)
    )
    hidden, first_back = jax.vjp(
        layer_norm, resid_first, gain_first.astype(jnp.float32), shift_first.astype(jnp.float32)
    )
    hidden_low = hidden.astype(jnp.bfloat16)
    upper = big_product(hidden_low, full_up) + bias_up.astype(jnp.float32)
    activated, gelu_back = jax.vjp(partial(jax.nn.gelu, approximate=False), upper)
    activated_low = activated.astype(jnp.bfloat16)
    resid_second = hidden + big_product(activated_low, full_down) + bias_down.astype(jnp.float32)
    normed, second_back = jax.vjp(
        layer_norm, resid_second, gain_second.astype(jnp.float32), shift_second.astype(jnp.float32)
    )
    layer_output = normed.astype(jnp.bfloat16)
    delta_second, second_gain_grad, second_shift_grad = second_back(
        output_cotangent.astype(jnp.float32)
    )
    delta_lower = delta_second.astype(jnp.bfloat16)
    down_grad = weight_grad(activated_low, delta_lower)
    down_bias_grad = bias_sum(delta_lower)
    delta_upper = gelu_back(back_product(delta_lower, full_down))[0].astype(jnp.bfloat16)
    up_grad = weight_grad(hidden_low, delta_upper)
    up_bias_grad = bias_sum(delta_upper)
    delta_hidden = back_product(delta_upper, full_up) + delta_second
    delta_first, first_gain_grad, first_shift_grad = first_back(delta_hidden)
    delta_proj = delta_first.astype(jnp.bfloat16)
    output_grad = weight_grad(attention, delta_proj)
    output_bias_grad = bias_sum(delta_proj)
    delta_attention = back_product(delta_proj, full_output)
    delta_queries, key_part, mixing_part, delta_ext, taps_part = near_back(delta_attention)
    (parts_own,) = exchange(seq, 6, (SCATTER, to_owners(mixing_part)))
    delta_mixing = as_pair(jnp.sum(parts_own.astype(jnp.float32), axis=0))
    query_own, key_own, far_own = mix_back(delta_mixing)
    inner_own = jnp.sum(far_own * distant_own, axis=-1).reshape(1, 2 * LANDMARKS)
    delta_fars, inners = exchange(
        seq,
        7,
        (GATHER, as_sides(far_own).astype(low)),
        (GATHER, jnp.pad(inner_own, ((0, 7), (0, 0)))),
    )
    far_query, far_keys, far_vals = far_back(
        query_marks, key_rows, value_float, peak, total, from_owners(delta_fars), rows_from_owners(inners, 0)
    )
    active = jnp.where(place_at < owners, 1.0, 0.0)

    def with_own(part, own):
        at = (own_row, 0, own_lane)
        held = lax.dynamic_slice(part, at, (1, LANDMARKS, 2 * HEAD_DIM))
        return lax.dynamic_update_slice(part, held + active * own[None], at)

    def by_owner(part):
        return jnp.swapaxes(part.reshape(batch_rows, seq, local_marks, features), 0, 1).astype(low)

    spread = jnp.stack(
        [by_owner(with_own(far_query, query_own)), by_owner(with_own(key_part, key_own))], axis=1
    )
    marks_parts, from_right, from_left = exchange(
        seq,
        8,
        (SCATTER, spread),
        (LAST, for_sending(delta_ext[:, :RIM])),
        (NEXT, for_sending(delta_ext[:, tokens + RIM :])),
    )
    from_right = jnp.where(place_at < seq - 1, from_right, jnp.zeros_like(from_right))
    from_left = jnp.where(place_at > 0, from_left, jnp.zeros_like(from_left))
    own_query, own_key = jnp.sum(marks_parts.astype(jnp.float32), axis=0)

    def spread_marks(marks):
        shaped = jnp.broadcast_to(
            (marks / segment)[:, :, None, :], (batch_rows, local_marks, segment, features)
        )
        return shaped.reshape(batch_rows, tokens, features)

    query_delta = (delta_queries + spread_marks(own_query)).astype(jnp.bfloat16)
    key_delta = (far_keys + spread_marks(own_key)).astype(jnp.bfloat16)
    value_sum = delta_ext[:, RIM : RIM + tokens] + far_vals
    value_sum = value_sum + jnp.pad(from_right, ((0, 0), (tokens - RIM, 0), (0, 0)))
    value_sum = value_sum + jnp.pad(from_left, ((0, 0), (0, tokens - RIM), (0, 0)))
    value_delta = value_sum.astype(jnp.bfloat16)
    query_grad = weight_grad(layer_input, query_delta)
    key_grad = weight_grad(layer_input, key_delta)
    value_grad = weight_grad(layer_input, value_delta)
    query_bias_grad = bias_sum(query_delta)
    value_bias_grad = bias_sum(value_delta)
    input_gradient = (
        back_product(query_delta, full_query)
        + back_product(key_delta, full_key)
        + back_product(value_delta, full_value)
        + delta_first
    )
    error_share = jnp.where(place_at < owners, error, 0.0) / (batch_rows * batch * HEADS)
    joined = jnp.concatenate([taps_part.reshape(-1), error_share[None]])
    joined = lax.psum(joined, BOTH)
    taps_gradient, pinv_error = joined[:-1].reshape(taps_part.shape), joined[-1]
    sizes = grid_of(batch, seq)
    grads = [
        grad.astype(jnp.bfloat16).reshape(sizes + (-1, grad.shape[-1]))
        for grad in (query_grad, key_grad, value_grad, output_grad, up_grad, down_grad)
    ]
    rows = [
        query_bias_grad,
        value_bias_grad,
        output_bias_grad,
        down_bias_grad,
        first_gain_grad,
        first_shift_grad,
        second_gain_grad,
        second_shift_grad,
    ]
    sums = jnp.concatenate(
        [
            jnp.swapaxes(jnp.stack(rows).reshape(8, batch * seq, own), 0, 1),
            up_bias_grad.reshape(batch * seq, wide, own),
        ],
        axis=1,
    )
    sums = jnp.pad(sums, ((0, 0), (0, 16 - sums.shape[1]), (0, 128 - own)))
    *owned, mine = scatter_grads(
        batch, seq, grads + [sums.reshape(sizes + (16, 128))], parts, orders, 2, 2
    )
    owned += [mine[0, :own], mine[1, :own], mine[2, :own], mine[8 : 8 + wide, :own].reshape(-1)]
    owned += [mine[at, :own] for at in range(3, 8)]
    return (
        layer_output,
        input_gradient,
        owned[0],
        owned[1],
        owned[2],
        owned[3],
        owned[4],
        owned[5],
        owned[6],
        owned[7],
        owned[8],
        owned[9],
        owned[10],
        owned[11],
        owned[12],
        owned[13],
        owned[14],
        taps_gradient,
        pinv_error,
    )


def solution(mesh):
    placed = (
        TOKENS,
        ROWS,
        ROWS,
        ROWS,
        ROWS,
        ROWS,
        ROWS,
        SPREAD,
        SPREAD,
        SPREAD,
        SPREAD,
        SPREAD,
        SPREAD,
        SPREAD,
        SPREAD,
        SPREAD,
        P(),
        TOKENS,
    )
    batch, seq = mesh.shape[BATCH], mesh.shape[SEQ]
    fits = seq == 16 and FEATURES % (8 * batch * seq) == 0
    return jax.shard_map(
        partial(local_fast, batch, seq) if fits else local,
        mesh=mesh,
        in_specs=placed,
        out_specs=(
            TOKENS,
            TOKENS,
            ROWS,
            ROWS,
            ROWS,
            ROWS,
            ROWS,
            ROWS,
            SPREAD,
            SPREAD,
            SPREAD,
            SPREAD,
            SPREAD,
            SPREAD,
            SPREAD,
            SPREAD,
            SPREAD,
            P(),
            P(),
        ),
        check_vma=False,
    )
```

profile of v0, /device:TPU:0, one launch (start us, length us, event | category | flops | bytes accessed | tf_op | source)
XLA Modules:
  0.0 617.3 jit_solution(13300804520636102335)
XLA Ops:
  2.8 82.0 %gather_weights.1 = (bf16[2,4,2,2,24,768]{5,4,3,2,1,0:T(8,128)(2,1)}, bf16[2,4,2,2,24,768]{5,4,3,2,1,0:T(8,128)(2,1)}, bf16[2,4,2,2,24,768]{5,4,3,2,1,0:T(8,128)...) custom-call(bf16[24,768]{1,0:T(8,128)(2,1)} %refs_0_.1, ...), custom_call_target="tpu_custom_call" | custom-call | tf_op jit(solution)/shard_map/gather_weights/pallas_call | solution.py:120
  88.8 2.8 broadcast_multiply_fusion.33
  94.4 1.8 fusion.51
  96.9 15.0 %exchange.6 = (bf16[16,2,2,4,768]{4,3,2,1,0:T(4,128)(2,1)}, bf16[2,16,768]{2,1,0:T(8,128)(2,1)}, bf16[2,16,768]{2,1,0:T(8,128)(2,1)}) custom-call(bf16[2,2,4,768]{3,2,1,0:T(4,128)(2,1)} %pad_maximum_fusion.5.refs_0_, bf16[2,16,768]{2,1,0:T(8,128)(2,1)} %get-tuple-element.210.refs_1_, bf16[2,16,768]{2,1,0:T(8,128)(2,1)} %get-tuple-element.209.refs_2_), custom_call_target="tpu_custom_call" | custom-call | tf_op jit(solution)/shard_map/exchange/pallas_call | solution.py:733
  118.8 1.5 copy.313
  121.8 1.6 fusion.167
  137.1 2.3 mul.1086
  139.4 1.5 copy.354
  141.0 2.7 fusion.166
  143.7 2.1 convolution_convert_fusion.1
  147.7 1.7 slice.330
  149.3 1.9 reshape.775
  151.2 1.7 pad_maximum_fusion.1.refs_0_
  157.5 14.1 %exchange.7 = (bf16[16,64,128]{2,1,0:T(8,128)(2,1)}, f32[16,8,128]{2,1,0:T(8,128)}) custom-call(bf16[16,64,128]{2,1,0:T(8,128)(2,1)} %pad_maximum_fusion.1.refs_0_, f32[16,8,128]{2,1,0:T(8,128)} %pad_maximum_fusion.4.refs_1_), custom_call_target="tpu_custom_call" | custom-call | tf_op jit(solution)/shard_map/exchange/pallas_call | solution.py:733
  171.6 2.5 reshape.819
  186.2 1.8 copy.302
  188.0 3.7 fusion.73
  191.7 1.6 copy.317
  197.7 13.7 %exchange.8 = (bf16[16,64,128]{2,1,0:T(8,128)(2,1)}, f32[16,8,128]{2,1,0:T(8,128)}) custom-call(bf16[64,128]{1,0:T(8,128)(2,1)} %convert_element_type.356.refs_0_, f32[8,128]{1,0:T(8,128)} %select_maximum_fusion.1.refs_1_), custom_call_target="tpu_custom_call" | custom-call | tf_op jit(solution)/shard_map/exchange/pallas_call | solution.py:733
  211.4 1.6 slice.334
  213.0 1.9 reshape.777
  214.8 1.9 copy.305
  216.7 9.3 %fusion.50 = bf16[2,128,12,64]{1,3,2,0:T(8,128)(2,1)} fusion(f32[2,160,12,64]{1,3,2,0:T(8,128)S(1)} %maximum_convert_fusion, f32[12]{0:T(128)} %get-tuple-element.119, f32[12]{0:T(128)} %get-tuple-element.120, f32[12]{0:T(128)} %get-tuple-element.121, f32[12]{0:T(128)} %get-tuple-element.122, f32[12]{0:T(128)} %get-tuple-element.123, ...), kind=kOutput, calls=%fused_computation.90 | convolution fusion | flops 164364288 | bytes 27342384 | tf_op jit(solution)/shard_map/jvp(shtm,shmd->sthd)/dot_general | solution.py:388
  226.0 1.9 fusion.168
  230.4 4.8 fusion.89
  235.2 8.2 %multiply_convert_fusion = (bf16[2,128,3072]{2,1,0:T(8,128)(2,1)S(1)}, f32[2,128,3072]{2,1,0:T(8,128)}) fusion(f32[2,128,3072]{2,1,0:T(8,128)S(1)} %get-tuple-element.247, u8[128,3072]{1,0:T(8,128)(4,1)S(1)} %get-tuple-element.72, u8[128,3072]{1,0:T(8,128)(4,1)S(1)} %get-tuple-element.71), kind=kLoop, calls=%fused_computation.14 | loop fusion | flops 55050240 | bytes 8650752 | tf_op jit(solution)/shard_map/convert_element_type | solution.py:939
  243.5 5.8 fusion.169
  250.8 2.2 fusion.76
  253.0 2.3 fusion.77
  257.2 3.2 convert_reduce_fusion.2
  261.2 7.0 %convert_reduce_fusion = (f32[3072]{0:T(1024)}, bf16[2,128,3072]{2,1,0:T(8,128)(2,1)S(1)}) fusion(f32[2,128,3072]{2,1,0:T(8,128)} %get-tuple-element.168, f32[2,128,3072]{2,1,0:T(8,128)} %copy-done.45, bf16[2,128,768]{2,1,0:T(8,128)(2,1)S(1)} %get-tuple-element.152, bf16[3072,768,1]{1,0,2:T(8,128)(2,1)} %bitcast.640), kind=kOutput, calls=%fused_computation.12 | convolution fusion | flops 1220539392 | bytes 12988416 | tf_op jit(solution)/shard_map/ste,de->std/dot_general | solution.py:448
  268.3 2.4 multiply_reduce_fusion.33
  272.1 5.5 multiply_reduce_fusion.31
  281.2 2.2 reshape.788
  284.0 1.9 convert_reduce_fusion.8
  285.9 1.9 convert_reduce_fusion.9
  287.8 2.1 convolution_convert_fusion
  291.5 12.6 %exchange.9 = bf16[16,64,128]{2,1,0:T(8,128)(2,1)} custom-call(bf16[16,64,128]{2,1,0:T(8,128)(2,1)} %pad_maximum_fusion.2.refs_0_), custom_call_target="tpu_custom_call" | custom-call | tf_op jit(solution)/shard_map/exchange/pallas_call | solution.py:733
  323.0 1.9 fusion.170
  330.3 13.3 %exchange.10 = (bf16[16,64,128]{2,1,0:T(8,128)(2,1)}, f32[16,8,128]{2,1,0:T(8,128)}) custom-call(bf16[64,128]{1,0:T(8,128)(2,1)} %copy.414.refs_0_, f32[8,128]{1,0:T(8,128)} %pad.229.refs_1_), custom_call_target="tpu_custom_call" | custom-call | tf_op jit(solution)/shard_map/exchange/pallas_call | solution.py:733
  346.4 1.5 slice_reduce_fusion.35
  350.7 1.6 slice.412
  352.3 1.9 reshape.785
  355.2 2.0 fusion.23
  361.9 1.9 pad_maximum_fusion.refs_0_
  363.9 1.8 broadcast_multiply_fusion
  367.5 14.0 %pad_add_fusion = f32[2,160,12,64]{1,3,2,0:T(8,128)} fusion(f32[2,128,12,64]{1,3,2,0:T(8,128)S(1)} %copy-done.89, f32[2,128,12,64]{1,3,2,0:T(8,128)S(1)} %copy-done.90, f32[2,128,12,64]{1,3,2,0:T(8,128)S(1)} %copy-done.91, f32[2,128,12,64]{1,3,2,0:T(8,128)S(1)} %get-tuple-element.174, f32[2,128,12,64]{1,3,2,0:T(8,128)S(1)} %get-tuple-element.175, ...), kind=kLoop, calls=%fused_computation.31 | loop fusion | flops 7864320 | bytes 26935296 | tf_op jit(solution)/shard_map/transpose(jvp())/add_any | solution.py:396
  381.5 1.8 copy.351
  384.1 15.9 %exchange.11 = (bf16[16,2,2,4,768]{4,3,2,1,0:T(4,128)(2,1)}, bf16[2,16,768]{2,1,0:T(8,128)(2,1)}, bf16[2,16,768]{2,1,0:T(8,128)(2,1)}) custom-call(bf16[16,2,2,4,768]{4,3,2,1,0:T(4,128)(2,1)} %pad_maximum_fusion.refs_0_, bf16[2,16,768]{2,1,0:T(8,128)(2,1)} %get-tuple-element.204.refs_1_, bf16[2,16,768]{2,1,0:T(8,128)(2,1)} %get-tuple-element.203.refs_2_), custom_call_target="tpu_custom_call" | custom-call | tf_op jit(solution)/shard_map/exchange/pallas_call | solution.py:733
  402.2 1.6 reshape.790
  403.8 1.5 copy.352
  405.3 4.5 convert_reduce_fusion.5
  412.1 1.8 reshape.791
  413.9 1.5 copy.355
  415.5 3.4 fusion.83
  420.3 1.9 fusion.94
  424.4 3.0 fusion.24
  430.7 1.6 bitcast_convert_fusion.3
  432.3 1.5 bitcast_convert_fusion.2
  433.8 3.7 bitcast_convert_fusion.1
  437.5 3.6 bitcast_convert_fusion
  466.7 84.0 %scatter_grads.1 = (f32[24,768]{1,0:T(8,128)S(1)}, f32[24,768]{1,0:T(8,128)S(1)}, f32[24,768]{1,0:T(8,128)S(1)}, f32[24,768]{1,0:T(8,128)S(1)}, f32[24,3072]{1,0...) custom-call(bf16[2,4,2,2,24,768]{5,4,3,2,1,0:T(8,128)(2,1)S(1)} %bitcast.524, ...), custom_call_target="tpu_custom_call" | custom-call | tf_op jit(solution)/shard_map/scatter_grads/pallas_call | solution.py:277
  558.5 13.7 %multiply_reduce_fusion.32 = (f32[12]{0:T(128)S(1)}, f32[12]{0:T(128)S(1)}, f32[12]{0:T(128)S(1)}, f32[12]{0:T(128)S(1)}, f32[12]{0:T(128)S(1)}, /*index=5*/f32[...) fusion(f32[2,128,12,64]{1,3,2,0:T(8,128)} %copy-done.17, ...), kind=kLoop, calls=%fused_computation.232 | loop fusion | flops 7077672 | bytes 14943072 | tf_op jit(solution)/shard_map/transpose(jvp())/reduce_sum | solution.py:396
  572.7 39.0 %psum.7 = f32[397]{0:T(512)S(1)} all-reduce(f32[397]{0:T(512)S(1)} %pad_maximum_fusion.6), channel_id=1, replica_groups=mesh['batch'=2,'seq'=16] {'batch','seq'}, use_global_device_ids=true, to_apply=%region_75.76 | all-reduce | flops 397 | bytes 3176 | tf_op jit(solution)/shard_map/psum | solution.py:1023
  (658 shorter events, 153.8 us)
Async XLA Ops:
  94.4 20.0 %copy-start.155 = (bf16[12,33]{1,0:T(8,128)(2,1)S(1)}, bf16[12,33]{1,0:T(8,128)(2,1)}, u32[]{:S(2)}) copy-start(bf16[12,33]{1,0:T(8,128)(2,1)} %param.34) | copy-start | bytes 2380
  114.4 157.6 %copy-start.13 = (f32[2,160,12,64]{1,3,2,0:T(8,128)}, f32[2,160,12,64]{1,3,2,0:T(8,128)S(1)}, u32[]{:S(2)}) copy-start(f32[2,160,12,64]{1,3,2,0:T(8,128)S(1)} %maximum_convert_fusion) | copy-start | bytes 2949124
  120.4 20.6 %copy-start.25 = (f32[2,64,12,64]{1,3,2,0:T(8,128)}, f32[2,64,12,64]{1,3,2,0:T(8,128)S(1)}, u32[]{:S(2)}) copy-start(f32[2,64,12,64]{1,3,2,0:T(8,128)S(1)} %copy.313) | copy-start | bytes 1179652
  125.4 9.2 %copy-start.118 = (f32[64,2,64]{2,1,0:T(2,128)}, f32[64,2,64]{2,1,0:T(2,128)S(1)}, u32[]{:S(2)}) copy-start(f32[64,2,64]{2,1,0:T(2,128)S(1)} %mul.1074) | copy-start | bytes 98308
  126.5 9.8 %copy-start.67 = (f32[1,2,16,4,768]{4,3,1,0,2:T(4,128)S(1)}, f32[1,2,16,4,768]{4,3,1,0,2:T(4,128)}, u32[]{:S(2)}) copy-start(f32[1,2,16,4,768]{4,3,1,0,2:T(4,128)} %get-tuple-element.206) | copy-start | bytes 1179652
  127.1 10.0 %copy-start.42 = (f32[2,64,64]{1,2,0:T(8,128)}, f32[2,64,64]{1,2,0:T(8,128)S(1)}, u32[]{:S(2)}) copy-start(f32[2,64,64]{1,2,0:T(8,128)S(1)} %get-tuple-element.236) | copy-start | bytes 98308
  127.1 10.0 %copy-start.125 = (f32[2,64]{1,0:T(2,128)}, f32[2,64]{1,0:T(2,128)S(1)}, u32[]{:S(2)}) copy-start(f32[2,64]{1,0:T(2,128)S(1)} %get-tuple-element.235) | copy-start | bytes 1540
  127.2 9.9 %copy-start.146 = (f32[2,64]{1,0:T(2,128)}, f32[2,64]{1,0:T(2,128)S(1)}, u32[]{:S(2)}) copy-start(f32[2,64]{1,0:T(2,128)S(1)} %get-tuple-element.114) | copy-start | bytes 1540
  127.2 9.9 %copy-start.147 = (f32[2,64]{1,0:T(2,128)}, f32[2,64]{1,0:T(2,128)S(1)}, u32[]{:S(2)}) copy-start(f32[2,64]{1,0:T(2,128)S(1)} %get-tuple-element.115) | copy-start | bytes 1540
  127.4 9.7 %copy-start.150 = (f32[2]{0:T(128)}, f32[2]{0:T(128)S(1)}, u32[]{:S(2)}) copy-start(f32[2]{0:T(128)S(1)} %reduce_max.55) | copy-start | bytes 28
  127.5 9.6 %copy-start.152 = (f32[2]{0:T(128)}, f32[2]{0:T(128)S(1)}, u32[]{:S(2)}) copy-start(f32[2]{0:T(128)S(1)} %reduce_max.56) | copy-start | bytes 28
  143.7 30.5 %copy-start.22 = (f32[2,12,64,128]{3,2,1,0:T(8,128)}, f32[2,12,64,128]{3,2,1,0:T(8,128)S(1)}, u32[]{:S(2)}) copy-start(f32[2,12,64,128]{3,2,1,0:T(8,128)S(1)} %get-tuple-element.240) | copy-start | bytes 2359300
  157.5 59.2 %copy-start.121 = (f32[2,12,128]{2,1,0:T(8,128)S(1)}, f32[2,12,128]{2,1,0:T(8,128)}, u32[]{:S(2)}) copy-start(f32[2,12,128]{2,1,0:T(8,128)} %get-tuple-element.243) | copy-start | bytes 36868
  174.2 42.6 %copy-start.30 = (f32[2,12,128,64]{2,3,1,0:T(8,128)S(1)}, f32[2,12,128,64]{2,3,1,0:T(8,128)}, u32[]{:S(2)}) copy-start(f32[2,12,128,64]{2,3,1,0:T(8,128)} %get-tuple-element.244) | copy-start | bytes 2359300
  228.0 42.8 %copy-start.14 = (f32[2,128,768]{2,1,0:T(8,128)}, f32[2,128,768]{2,1,0:T(8,128)S(1)}, u32[]{:S(2)}) copy-start(f32[2,128,768]{2,1,0:T(8,128)S(1)} %get-tuple-element.246) | copy-start | bytes 2359300
  230.4 13.0 %copy-start.137 = (f32[2,128]{1,0:T(2,128)}, f32[2,128]{1,0:T(2,128)S(1)}, u32[]{:S(2)}) copy-start(f32[2,128]{1,0:T(2,128)S(1)} %fusion.148) | copy-start | bytes 3076
  257.2 11.0 %slice-start = ((s8[4718592]{0:T(1024)(128)(4,1)}), s8[4194304]{0:T(1024)(128)(4,1)S(1)}, s32[]{:S(2)}) async-start(s8[4718592]{0:T(1024)(128)(4,1)} %bitcast.636), calls=%async_computation | async-start | bytes 8388608
  277.5 88.2 %copy-start.17 = (f32[2,128,12,64]{1,3,2,0:T(8,128)}, f32[2,128,12,64]{1,3,2,0:T(8,128)S(1)}, u32[]{:S(2)}) copy-start(f32[2,128,12,64]{1,3,2,0:T(8,128)S(1)} %get-tuple-element.259) | copy-start | bytes 2359300
  278.3 9.5 %copy-start.32 = (f32[2,12,128,64]{2,3,1,0:T(8,128)S(1)}, f32[2,12,128,64]{2,3,1,0:T(8,128)}, u32[]{:S(2)}) copy-start(f32[2,12,128,64]{2,3,1,0:T(8,128)} %get-tuple-element.244) | copy-start | bytes 2359300
  283.4 21.8 %copy-start.88 = (f32[2,64,64]{1,2,0:T(8,128)S(1)}, f32[2,64,64]{1,2,0:T(8,128)}, u32[]{:S(2)}) copy-start(f32[2,64,64]{1,2,0:T(8,128)} %copy.317) | copy-start | bytes 98308
  287.7 17.9 %copy-start.78 = (f32[2,64,64]{2,1,0:T(8,128)S(1)}, f32[2,64,64]{2,1,0:T(8,128)}, u32[]{:S(2)}) copy-start(f32[2,64,64]{2,1,0:T(8,128)} %copy-done.77) | copy-start | bytes 98308
  287.7 19.3 %copy-start.62 = (f32[2,64,64]{2,1,0:T(8,128)S(1)}, f32[2,64,64]{2,1,0:T(8,128)}, u32[]{:S(2)}) copy-start(f32[2,64,64]{2,1,0:T(8,128)} %copy-done.61) | copy-start | bytes 98308
  287.7 19.7 %copy-start.34 = (f32[64,64]{1,0:T(8,128)S(1)}, f32[64,64]{1,0:T(8,128)}, u32[]{:S(2)}) copy-start(f32[64,64]{1,0:T(8,128)} %copy-done.33) | copy-start | bytes 49156
  287.7 20.2 %copy-start.43 = (f32[2,64,64]{1,2,0:T(8,128)S(1)}, f32[2,64,64]{1,2,0:T(8,128)}, u32[]{:S(2)}) copy-start(f32[2,64,64]{1,2,0:T(8,128)} %copy-done.42) | copy-start | bytes 98308
  289.9 15.5 %copy-start.101 = (f32[2,64,64]{2,1,0:T(8,128)S(1)}, f32[2,64,64]{2,1,0:T(8,128)}, u32[]{:S(2)}) copy-start(f32[2,64,64]{2,1,0:T(8,128)} %copy-done.100) | copy-start | bytes 98308
  289.9 18.3 %copy-start.99 = (f32[2,64,64]{2,1,0:T(8,128)S(1)}, f32[2,64,64]{2,1,0:T(8,128)}, u32[]{:S(2)}) copy-start(f32[2,64,64]{2,1,0:T(8,128)} %copy-done.98) | copy-start | bytes 98308
  289.9 18.5 %copy-start.86 = (f32[2,64,64]{2,1,0:T(8,128)S(1)}, f32[2,64,64]{2,1,0:T(8,128)}, u32[]{:S(2)}) copy-start(f32[2,64,64]{2,1,0:T(8,128)} %copy-done.85) | copy-start | bytes 98308
  289.9 19.9 %copy-start.60 = (f32[2,64,64]{2,1,0:T(8,128)S(1)}, f32[2,64,64]{2,1,0:T(8,128)}, u32[]{:S(2)}) copy-start(f32[2,64,64]{2,1,0:T(8,128)} %copy-done.59) | copy-start | bytes 98308
  290.3 20.6 %copy-start.97 = (f32[2,64,64]{2,1,0:T(8,128)S(1)}, f32[2,64,64]{2,1,0:T(8,128)}, u32[]{:S(2)}) copy-start(f32[2,64,64]{2,1,0:T(8,128)} %copy-done.96) | copy-start | bytes 98308
  290.3 20.8 %copy-start.83 = (f32[2,64,64]{2,1,0:T(8,128)S(1)}, f32[2,64,64]{2,1,0:T(8,128)}, u32[]{:S(2)}) copy-start(f32[2,64,64]{2,1,0:T(8,128)} %copy-done.82) | copy-start | bytes 98308
  290.4 22.1 %copy-start.58 = (f32[2,64,64]{2,1,0:T(8,128)S(1)}, f32[2,64,64]{2,1,0:T(8,128)}, u32[]{:S(2)}) copy-start(f32[2,64,64]{2,1,0:T(8,128)} %copy-done.57) | copy-start | bytes 98308
  290.8 22.9 %copy-start.95 = (f32[2,64,64]{2,1,0:T(8,128)S(1)}, f32[2,64,64]{2,1,0:T(8,128)}, u32[]{:S(2)}) copy-start(f32[2,64,64]{2,1,0:T(8,128)} %copy-done.94) | copy-start | bytes 98308
  291.5 22.4 %copy-start.80 = (f32[2,64,64]{2,1,0:T(8,128)S(1)}, f32[2,64,64]{2,1,0:T(8,128)}, u32[]{:S(2)}) copy-start(f32[2,64,64]{2,1,0:T(8,128)} %copy-done.79) | copy-start | bytes 98308
  291.5 22.7 %copy-start.110 = (f32[2,64,64]{2,1,0:T(8,128)S(1)}, f32[2,64,64]{2,1,0:T(8,128)}, u32[]{:S(2)}) copy-start(f32[2,64,64]{2,1,0:T(8,128)} %copy-done.109) | copy-start | bytes 98308
  291.5 22.9 %copy-start.56 = (f32[2,64,64]{2,1,0:T(8,128)S(1)}, f32[2,64,64]{2,1,0:T(8,128)}, u32[]{:S(2)}) copy-start(f32[2,64,64]{2,1,0:T(8,128)} %copy-done.55) | copy-start | bytes 98308
  305.2 10.2 %copy-start.102 = (f32[64,2,64]{2,1,0:T(2,128)}, f32[64,2,64]{2,1,0:T(2,128)S(1)}, u32[]{:S(2)}) copy-start(f32[64,2,64]{2,1,0:T(2,128)S(1)} %reshape.783) | copy-start | bytes 98308
  305.7 9.9 %copy-start.93 = (f32[2,64,64]{2,1,0:T(8,128)S(1)}, f32[2,64,64]{2,1,0:T(8,128)}, u32[]{:S(2)}) copy-start(f32[2,64,64]{2,1,0:T(8,128)} %copy-done.92) | copy-start | bytes 98308
  306.0 9.8 %copy-start.104 = (f32[2,64,64]{2,1,0:T(8,128)S(1)}, f32[2,64,64]{2,1,0:T(8,128)}, u32[]{:S(2)}) copy-start(f32[2,64,64]{2,1,0:T(8,128)} %copy-done.103) | copy-start | bytes 98308
  307.1 9.0 %copy-start.108 = (f32[2,64,64]{2,1,0:T(8,128)S(1)}, f32[2,64,64]{2,1,0:T(8,128)}, u32[]{:S(2)}) copy-start(f32[2,64,64]{2,1,0:T(8,128)} %copy-done.107) | copy-start | bytes 98308
  319.4 35.8 %copy-start.23 = (f32[2,12,64,128]{3,2,1,0:T(8,128)S(1)}, f32[2,12,64,128]{3,2,1,0:T(8,128)}, u32[]{:S(2)}) copy-start(f32[2,12,64,128]{3,2,1,0:T(8,128)} %copy-done.22) | copy-start | bytes 2359300
  323.0 34.3 %copy-start.26 = (f32[2,128,768]{1,2,0:T(8,128)S(1)}, f32[2,128,768]{1,2,0:T(8,128)}, u32[]{:S(2)}) copy-start(f32[2,128,768]{1,2,0:T(8,128)} %get-tuple-element.237) | copy-start | bytes 2359300
  383.3 17.9 %copy-start.20 = (f32[2,160,768]{2,1,0:T(8,128)}, f32[2,160,768]{2,1,0:T(8,128)S(1)}, u32[]{:S(2)}) copy-start(f32[2,160,768]{2,1,0:T(8,128)S(1)} %copy.351) | copy-start | bytes 2949124
  437.5 24.7 %copy-start.132 = (f32[768]{0:T(1024)S(1)}, f32[768]{0:T(1024)}, u32[]{:S(2)}) copy-start(f32[768]{0:T(1024)} %get-tuple-element.113) | copy-start | bytes 9220
  558.3 13.9 %copy-start.175 = (f32[12]{0:T(128)S(1)}, f32[12]{0:T(128)}, u32[]{:S(2)}) copy-start(f32[12]{0:T(128)} %get-tuple-element.91) | copy-start | bytes 148
  558.3 13.9 %copy-start.176 = (f32[12]{0:T(128)S(1)}, f32[12]{0:T(128)}, u32[]{:S(2)}) copy-start(f32[12]{0:T(128)} %get-tuple-element.92) | copy-start | bytes 148
  558.3 13.9 %copy-start.177 = (f32[12]{0:T(128)S(1)}, f32[12]{0:T(128)}, u32[]{:S(2)}) copy-start(f32[12]{0:T(128)} %get-tuple-element.93) | copy-start | bytes 148
  558.3 13.9 %copy-start.178 = (f32[12]{0:T(128)S(1)}, f32[12]{0:T(128)}, u32[]{:S(2)}) copy-start(f32[12]{0:T(128)} %get-tuple-element.94) | copy-start | bytes 148
  558.4 13.9 %copy-start.179 = (f32[12]{0:T(128)S(1)}, f32[12]{0:T(128)}, u32[]{:S(2)}) copy-start(f32[12]{0:T(128)} %get-tuple-element.95) | copy-start | bytes 148
  558.4 13.9 %copy-start.180 = (f32[12]{0:T(128)S(1)}, f32[12]{0:T(128)}, u32[]{:S(2)}) copy-start(f32[12]{0:T(128)} %get-tuple-element.96) | copy-start | bytes 148
  558.4 13.9 %copy-start.181 = (f32[12]{0:T(128)S(1)}, f32[12]{0:T(128)}, u32[]{:S(2)}) copy-start(f32[12]{0:T(128)} %get-tuple-element.97) | copy-start | bytes 148
  558.4 13.9 %copy-start.182 = (f32[12]{0:T(128)S(1)}, f32[12]{0:T(128)}, u32[]{:S(2)}) copy-start(f32[12]{0:T(128)} %get-tuple-element.98) | copy-start | bytes 148
  558.4 13.9 %copy-start.183 = (f32[12]{0:T(128)S(1)}, f32[12]{0:T(128)}, u32[]{:S(2)}) copy-start(f32[12]{0:T(128)} %get-tuple-element.99) | copy-start | bytes 148
  558.4 13.9 %copy-start.184 = (f32[12]{0:T(128)S(1)}, f32[12]{0:T(128)}, u32[]{:S(2)}) copy-start(f32[12]{0:T(128)} %get-tuple-element.100) | copy-start | bytes 148
  558.4 13.9 %copy-start.185 = (f32[12]{0:T(128)S(1)}, f32[12]{0:T(128)}, u32[]{:S(2)}) copy-start(f32[12]{0:T(128)} %get-tuple-element.101) | copy-start | bytes 148
  558.4 13.9 %copy-start.186 = (f32[12]{0:T(128)S(1)}, f32[12]{0:T(128)}, u32[]{:S(2)}) copy-start(f32[12]{0:T(128)} %get-tuple-element.102) | copy-start | bytes 148
  558.4 13.9 %copy-start.187 = (f32[12]{0:T(128)S(1)}, f32[12]{0:T(128)}, u32[]{:S(2)}) copy-start(f32[12]{0:T(128)} %get-tuple-element.103) | copy-start | bytes 148
  558.4 13.9 %copy-start.188 = (f32[12]{0:T(128)S(1)}, f32[12]{0:T(128)}, u32[]{:S(2)}) copy-start(f32[12]{0:T(128)} %get-tuple-element.104) | copy-start | bytes 148
  558.5 13.9 %copy-start.189 = (f32[12]{0:T(128)S(1)}, f32[12]{0:T(128)}, u32[]{:S(2)}) copy-start(f32[12]{0:T(128)} %get-tuple-element.105) | copy-start | bytes 148
  558.5 54.5 %copy-start.12 = (f32[24,768]{1,0:T(8,128)S(1)}, f32[24,768]{1,0:T(8,128)}, u32[]{:S(2)}) copy-start(f32[24,768]{1,0:T(8,128)} %copy-done.11) | copy-start | bytes 221188
  558.5 55.1 %copy-start.10 = (f32[24,768]{1,0:T(8,128)S(1)}, f32[24,768]{1,0:T(8,128)}, u32[]{:S(2)}) copy-start(f32[24,768]{1,0:T(8,128)} %copy-done.9) | copy-start | bytes 221188
  558.5 55.7 %copy-start.8 = (f32[24,768]{1,0:T(8,128)S(1)}, f32[24,768]{1,0:T(8,128)}, u32[]{:S(2)}) copy-start(f32[24,768]{1,0:T(8,128)} %copy-done.7) | copy-start | bytes 221188
  558.5 56.3 %copy-start.6 = (f32[24,768]{1,0:T(8,128)S(1)}, f32[24,768]{1,0:T(8,128)}, u32[]{:S(2)}) copy-start(f32[24,768]{1,0:T(8,128)} %copy-done.5) | copy-start | bytes 221188
  558.5 57.0 %copy-start.4 = (f32[24,3072]{1,0:T(8,128)S(1)}, f32[24,3072]{1,0:T(8,128)}, u32[]{:S(2)}) copy-start(f32[24,3072]{1,0:T(8,128)} %copy-done.3) | copy-start | bytes 884740
  558.5 57.7 %copy-start.2 = (f32[96,768]{1,0:T(8,128)S(1)}, f32[96,768]{1,0:T(8,128)}, u32[]{:S(2)}) copy-start(f32[96,768]{1,0:T(8,128)} %copy-done.1) | copy-start | bytes 884740
  (135 other events, 512.7 us)
where the time goes:
time: 628 us; the launch traced here: 617 us
  Pallas kernels  251 us (40%)
  local copies, waits for them, and re-layouts  129 us (21%)
  matrix products  110 us (18%)
  other arithmetic  83.4 us (13%)
  blocking collectives  39 us (6%)
    pallas_call x6, Pallas kernels, exchange(): pl.pallas_call(partial(exchange_kernel, ways), out_shape=[jax.ShapeDtypeS...  84.5 us
    pallas_call x1, Pallas kernels, scatter_grads(): pl.pallas_call(partial(scatter_kernel, batch, seq, parts, orders, unit, n...  84 us
    pallas_call x1, Pallas kernels, gather_weights(): pl.pallas_call(partial(gather_kernel, batch, seq, parts, orders, unit, n)...  82 us
    psum x1, blocking collectives, local_fast(): joined = lax.psum(joined, BOTH)  39 us
    unnamed x416, local copies, waits for them, and re-layouts  28.7 us
    dot_general x6, matrix products, back_product(): jnp.einsum('ste,de->std', delta, weight, preferred_element_type=jnp.float32)  20.7 us
    dot_general x6, matrix products, big_product(): jnp.einsum('std,de->ste', left, right, preferred_element_type=jnp.float32)  18.5 us
    add_any x1, other arithmetic, near_mix(): window[:, tap_index:tap_index + length]  14 us

commit v1 on v0

--- a/solution.py
+++ b/solution.py
@@ -12,6 +12,7 @@
 BOTH = (BATCH, SEQ)
 ROWS, SPREAD, TOKENS = P(BOTH, None), P(BOTH), P(BATCH, SEQ, None)
 GATHER, SCATTER, NEXT, LAST = range(4)
+NEAR_SCORES, NEAR_OUT = "sthd,smhd->shtm", "shtm,shmd->sthd"
 ALL = slice(None)
 LAG = 1
 
@@ -231,9 +232,13 @@
     def reduce_line(part):
         arrive(part, 3)
         index, rows, cols = parts[part]
-        value = mine(part, "")[...].astype(jnp.float32)
-        for step, _ in g.others("z"):
-            value += from_line[part][step - 1].astype(jnp.float32)
+        own, size = mine(part, "")[...].astype(jnp.float32), g.sizes["z"]
+        value = None
+        for z in range(size):
+            step = lax.rem(g.at["z"] - z + size, size)
+            came = from_line[part][lax.rem(step + size - 2, size - 1)].astype(jnp.float32)
+            term = jnp.where(step == 0, own, came)
+            value = term if value is None else value + term
         outs[index][rows, cols] = value
 
     units = [range(at, min(at + unit, count)) for at in range(0, count, unit)]
@@ -379,14 +384,14 @@
 def near_mix(queries, mark_key, mixing_result, value_ext, taps):
     scale = HEAD_DIM ** (-0.25)
     scores = jnp.einsum(
-        "sthd,smhd->shtm",
+        NEAR_SCORES,
         split_heads(queries) * scale,
         split_heads(mark_key) * scale,
         precision=highest_precision,
     )
     nearby_part = jax.nn.softmax(scores, axis=-1)
     attended_output = jnp.einsum(
-        "shtm,shmd->sthd", nearby_part, mixing_result, precision=highest_precision
+        NEAR_OUT, nearby_part, mixing_result, precision=highest_precision
     )
     window = split_heads(value_ext)
     length = queries.shape[1]
@@ -777,6 +782,24 @@
     )
 
 
+def near_mix_banded(queries, mark_key, mixing_result, value_ext, taps):
+    scale = HEAD_DIM ** (-0.25)
+    scores = jnp.einsum(
+        NEAR_SCORES, split_heads(queries) * scale, split_heads(mark_key) * scale, precision=highest_precision
+    )
+    nearby_part = jax.nn.softmax(scores, axis=-1)
+    attended_output = jnp.einsum(NEAR_OUT, nearby_part, mixing_result, precision=highest_precision)
+    length, reach = queries.shape[1], value_ext.shape[1]
+    shape = (KERNEL, length, reach)
+    tap, token, source = (lax.broadcasted_iota(jnp.int32, shape, at) for at in range(3))
+    chosen = (source - token == tap).astype(jnp.float32)
+    banded = jnp.einsum("hj,jtu->htu", taps, chosen, precision=highest_precision)
+    attended_output = attended_output + jnp.einsum(
+        "htu,suhd->sthd", banded, split_heads(value_ext), precision=highest_precision
+    )
+    return attended_output.reshape(queries.shape)
+
+
 def local_fast(
     batch,
     seq,
@@ -922,7 +945,7 @@
     mixing_result = from_owners(mixings)
     peak, total = rows_from_owners(stats, 0), rows_from_owners(stats, 1)
     attended_output, near_back = jax.vjp(
-        near_mix, queries, key_marks, mixing_result, ext_float, taps
+        near_mix_banded, queries, key_marks, mixing_result, ext_float, taps
     )
     attention = attended_output.astype(jnp.bfloat16)
     resid_first = (
@@ -1020,8 +1043,7 @@
     )
     error_share = jnp.where(place_at < owners, error, 0.0) / (batch_rows * batch * HEADS)
     joined = jnp.concatenate([taps_part.reshape(-1), error_share[None]])
-    joined = lax.psum(joined, BOTH)
-    taps_gradient, pinv_error = joined[:-1].reshape(taps_part.shape), joined[-1]
+    joined = jnp.pad(joined, (0, 4 * 128 - joined.shape[0])).reshape(1, 4, 128)
     sizes = grid_of(batch, seq)
     grads = [
         grad.astype(jnp.bfloat16).reshape(sizes + (-1, grad.shape[-1]))
@@ -1044,10 +1066,14 @@
         ],
         axis=1,
     )
-    sums = jnp.pad(sums, ((0, 0), (0, 16 - sums.shape[1]), (0, 128 - own)))
+    sums = jnp.pad(sums, ((0, 0), (0, 0), (0, 128 - own)))
+    sums = jnp.concatenate([sums, jnp.broadcast_to(joined, (batch * seq, 4, 128))], axis=1)
     *owned, mine = scatter_grads(
         batch, seq, grads + [sums.reshape(sizes + (16, 128))], parts, orders, 2, 2
     )
+    joined = mine[12:].reshape(-1)
+    taps_gradient = joined[: HEADS * KERNEL].reshape(taps_part.shape)
+    pinv_error = joined[HEADS * KERNEL]
     owned += [mine[0, :own], mine[1, :own], mine[2, :own], mine[8 : 8 + wide, :own].reshape(-1)]
     owned += [mine[at, :own] for at in range(3, 8)]
     return (

time: 628 us -> 501 us (0.80)
  local copies, waits for them, and re-layouts: 129 us -> 82.4 us
  other arithmetic: 83.4 us -> 43.2 us
  blocking collectives: 39 us -> 0 us
    psum x1 -> x0, blocking collectives: 39 us -> none  [local_fast(): joined = lax.psum(joined, BOTH)]
    unnamed x416 -> x257, local copies, waits for them, and re-layouts: 28.7 us -> 12.6 us
    add_any x2 -> x0, other arithmetic: 14.1 us -> none  [the longest x1 14 us: near_mix(): window[:, tap_index:tap_index + length]]
    reduce_sum x1 -> x0, other arithmetic: 13.7 us -> none  [near_mix(): taps[:, tap_index][:, None] * window[:, tap_index:tap_index + length]]
    another operation x9, local copies, waits for them, and re-layouts: 10.9 us -> 0.63 us  [local_fast(): jnp.stack(rows).reshape(8, batch * seq, own)]
    dot_general x6 -> x11, matrix products: 19.4 us -> 23.1 us  [the longest x3 9.69 us: near_mix_banded(): jnp.einsum(NEAR_SCORES, split_heads(queries) * scale, split_heads(mark_ke...]
where the time goes in v1:
time: 501 us; the launch traced here: 494 us
  Pallas kernels  251 us (50%)
  matrix products  113 us (23%)
  local copies, waits for them, and re-layouts  82.4 us (16%)
  other arithmetic  43.2 us (9%)
    pallas_call x1, Pallas kernels, scatter_grads(): pl.pallas_call(partial(scatter_kernel, batch, seq, parts, orders, unit, n...  84.6 us
    pallas_call x6, Pallas kernels, exchange(): pl.pallas_call(partial(exchange_kernel, ways), out_shape=[jax.ShapeDtypeS...  84.4 us
    pallas_call x1, Pallas kernels, gather_weights(): pl.pallas_call(partial(gather_kernel, batch, seq, parts, orders, unit, n)...  82 us
    dot_general x6, matrix products, big_product(): jnp.einsum('std,de->ste', left, right, preferred_element_type=jnp.float32)  17.2 us
    dot_general x36, matrix products, pseudo_inverse(): jnp.matmul(product, inner, precision=highest_precision)  15.3 us
    dot_general x6, matrix products, back_product(): jnp.einsum('ste,de->std', delta, weight, preferred_element_type=jnp.float32)  14.9 us
    unnamed x257, local copies, waits for them, and re-layouts  12.6 us
    dot_general x6, matrix products, weight_grad(): jnp.einsum('std,ste->de', left, right, preferred_element_type=jnp.float32)  10.9 us

profile of v1, /device:TPU:0, one launch (start us, length us, event | category | flops | bytes accessed | tf_op | source)
XLA Modules:
  0.0 494.0 jit_solution(15863338814551514785)
XLA Ops:
  2.8 82.0 %gather_weights.1 = (bf16[2,4,2,2,24,768]{5,4,3,2,1,0:T(8,128)(2,1)}, bf16[2,4,2,2,24,768]{5,4,3,2,1,0:T(8,128)(2,1)}, bf16[2,4,2,2,24,768]{5,4,3,2,1,0:T(8,128)...) custom-call(bf16[24,768]{1,0:T(8,128)(2,1)} %refs_0_.1, ...), custom_call_target="tpu_custom_call" | custom-call | tf_op jit(solution)/shard_map/gather_weights/pallas_call | solution.py:121
  86.7 3.0 broadcast_multiply_fusion
  89.7 1.4 copy.291
  91.2 1.4 broadcast_multiply_fusion.1
  93.8 1.8 fusion.22
  96.2 15.3 %exchange.6 = (bf16[16,2,2,4,768]{4,3,2,1,0:T(4,128)(2,1)}, bf16[2,16,768]{2,1,0:T(8,128)(2,1)}, bf16[2,16,768]{2,1,0:T(8,128)(2,1)}) custom-call(bf16[2,2,4,768]{3,2,1,0:T(4,128)(2,1)} %pad_maximum_fusion.6.refs_0_, bf16[2,16,768]{2,1,0:T(8,128)(2,1)} %get-tuple-element.111.refs_1_, bf16[2,16,768]{2,1,0:T(8,128)(2,1)} %get-tuple-element.110.refs_2_), custom_call_target="tpu_custom_call" | custom-call | tf_op jit(solution)/shard_map/exchange/pallas_call | solution.py:738
  111.5 2.0 broadcast_multiply_fusion.2
  114.3 3.0 fusion.147
  121.3 13.8 %exchange.7 = (bf16[16,64,128]{2,1,0:T(8,128)(2,1)}, f32[16,8,128]{2,1,0:T(8,128)}) custom-call(bf16[16,64,128]{2,1,0:T(8,128)(2,1)} %pad_maximum_fusion.2.refs_0_, f32[16,8,128]{2,1,0:T(8,128)} %pad_maximum_fusion.5.refs_1_), custom_call_target="tpu_custom_call" | custom-call | tf_op jit(solution)/shard_map/exchange/pallas_call | solution.py:738
  138.0 1.5 reshape.594
  153.3 13.7 %exchange.8 = (bf16[16,64,128]{2,1,0:T(8,128)(2,1)}, f32[16,8,128]{2,1,0:T(8,128)}) custom-call(bf16[64,128]{1,0:T(8,128)(2,1)} %convert_element_type.354.refs_0_, f32[8,128]{1,0:T(8,128)} %select_maximum_fusion.2.refs_1_), custom_call_target="tpu_custom_call" | custom-call | tf_op jit(solution)/shard_map/exchange/pallas_call | solution.py:738
  168.8 1.3 mul.468
  170.2 1.5 copy.322
  171.8 2.9 fusion.152
  176.0 1.4 convolution_bitcast_fusion.2
  179.5 2.3 fusion.21
  181.9 1.9 fusion.149
  186.5 4.8 fusion.67
  191.3 8.6 %multiply_convert_fusion = (bf16[2,128,3072]{2,1,0:T(8,128)(2,1)}, f32[2,128,3072]{2,1,0:T(8,128)}) fusion(f32[2,128,3072]{2,1,0:T(8,128)S(1)} %get-tuple-element.148, u8[128,3072]{1,0:T(8,128)(4,1)S(1)} %get-tuple-element.72, u8[128,3072]{1,0:T(8,128)(4,1)S(1)} %get-tuple-element.71), kind=kLoop, calls=%fused_computation.17 | loop fusion | flops 55050240 | bytes 8650752 | tf_op jit(solution)/shard_map/convert_element_type | solution.py:962
  200.6 4.4 fusion.150
  209.0 2.6 convert_reduce_fusion.2
  211.6 7.1 %convert_reduce_fusion = (f32[3072]{0:T(1024)}, bf16[2,128,3072]{2,1,0:T(8,128)(2,1)S(1)}) fusion(f32[2,128,3072]{2,1,0:T(8,128)} %get-tuple-element.102, f32[2,128,3072]{2,1,0:T(8,128)} %copy-done.22, bf16[2,128,768]{2,1,0:T(8,128)(2,1)S(1)} %get-tuple-element.86, bf16[3072,768,1]{1,0,2:T(8,128)(2,1)} %bitcast.537), kind=kOutput, calls=%fused_computation.15 | convolution fusion | flops 1220539392 | bytes 12988416 | tf_op jit(solution)/shard_map/ste,de->std/dot_general | solution.py:453
  218.7 2.3 multiply_reduce_fusion
  222.9 1.4 convolution_convert_fusion
  225.4 1.9 reshape.556
  227.3 1.6 slice.185
  229.0 1.7 slice.150
  230.6 1.7 pad_maximum_fusion.3.refs_0_
  232.3 12.5 %exchange.9 = bf16[16,64,128]{2,1,0:T(8,128)(2,1)} custom-call(bf16[16,64,128]{2,1,0:T(8,128)(2,1)} %pad_maximum_fusion.3.refs_0_), custom_call_target="tpu_custom_call" | custom-call | tf_op jit(solution)/shard_map/exchange/pallas_call | solution.py:738
  247.7 1.4 fusion.90
  252.4 13.3 %exchange.10 = (bf16[16,64,128]{2,1,0:T(8,128)(2,1)}, f32[16,8,128]{2,1,0:T(8,128)}) custom-call(bf16[64,128]{1,0:T(8,128)(2,1)} %copy.425.refs_0_, f32[8,128]{1,0:T(8,128)} %pad.35.refs_1_), custom_call_target="tpu_custom_call" | custom-call | tf_op jit(solution)/shard_map/exchange/pallas_call | solution.py:738
  265.7 1.6 slice.151
  267.3 1.9 reshape.559
  269.2 1.8 copy.327
  272.7 2.9 fusion.72
  275.6 2.3 copy.371
  304.6 2.1 fusion.14
  307.5 2.6 convolution_multiply_fusion.2
  311.7 1.4 copy.352
  313.1 2.2 dynamic_update_slice.6
  317.3 1.6 multiply_reduce_fusion.1
  319.0 2.8 fusion.16
  323.4 1.4 add_dynamic-update-slice_fusion
  326.1 1.9 pad_maximum_fusion.1.refs_0_
  328.0 3.4 convolution_bitcast_fusion
  331.4 1.3 copy.362
  332.7 1.8 copy.363
  335.2 15.9 %exchange.11 = (bf16[16,2,2,4,768]{4,3,2,1,0:T(4,128)(2,1)}, bf16[2,16,768]{2,1,0:T(8,128)(2,1)}, bf16[2,16,768]{2,1,0:T(8,128)(2,1)}) custom-call(bf16[16,2,2,4,768]{4,3,2,1,0:T(4,128)(2,1)} %pad_maximum_fusion.1.refs_0_, bf16[2,16,768]{2,1,0:T(8,128)(2,1)} %get-tuple-element.105.refs_1_, bf16[2,16,768]{2,1,0:T(8,128)(2,1)} %get-tuple-element.104.refs_2_), custom_call_target="tpu_custom_call" | custom-call | tf_op jit(solution)/shard_map/exchange/pallas_call | solution.py:738
  351.9 2.0 convert_reduce_fusion.4
  355.3 1.8 reshape.564
  357.2 3.0 copy.364
  360.2 3.9 convert_reduce_fusion.5
  367.5 1.9 fusion.44
  371.5 5.1 %bitcast_convert_fusion = bf16[3072,768]{1,0:T(8,128)(2,1)} fusion(bf16[2,128,3072]{2,1,0:T(8,128)(2,1)} %get-tuple-element.101, bf16[2,128,768]{2,1,0:T(8,128)(2,1)S(1)} %copy-done.31), kind=kOutput, calls=%fused_computation.2 | convolution fusion | flops 1210318848 | bytes 6684672 | tf_op jit(solution)/shard_map/std,ste->de/dot_general | solution.py:449
  376.6 3.7 bitcast_convert_fusion.1
  381.8 2.9 reshape.565
  384.7 3.1 copy.367
  387.8 3.4 fusion.60
  391.2 1.4 copy.374
  393.2 2.3 copy.372
  397.7 84.6 %scatter_grads.1 = (f32[24,768]{1,0:T(8,128)S(1)}, f32[24,768]{1,0:T(8,128)S(1)}, f32[24,768]{1,0:T(8,128)S(1)}, f32[24,768]{1,0:T(8,128)S(1)}, f32[24,3072]{1,0...) custom-call(bf16[2,4,2,2,24,768]{5,4,3,2,1,0:T(8,128)(2,1)S(1)} %bitcast.455, ...), custom_call_target="tpu_custom_call" | custom-call | tf_op jit(solution)/shard_map/scatter_grads/pallas_call | solution.py:282
  484.8 2.0 fusion.166
  486.8 1.6 convolution_add_fusion.2
  488.4 1.4 fusion.15
  (496 shorter events, 101.1 us)
Async XLA Ops:
  0.7 177.2 %copy-start = (bf16[12,33]{1,0:T(8,128)(2,1)S(1)}, bf16[12,33]{1,0:T(8,128)(2,1)}, u32[]{:S(2)}) copy-start(bf16[12,33]{1,0:T(8,128)(2,1)} %param.34) | copy-start | bytes 2380
  95.5 23.1 %copy-start.28 = (bf16[2,128,768]{2,1,0:T(8,128)(2,1)}, bf16[2,128,768]{2,1,0:T(8,128)(2,1)S(1)}, u32[]{:S(2)}) copy-start(bf16[2,128,768]{2,1,0:T(8,128)(2,1)S(1)} %fusion.22) | copy-start | bytes 1179652
  140.9 11.3 %copy-start.45 = (f32[2,64,64]{1,2,0:T(8,128)}, f32[2,64,64]{1,2,0:T(8,128)S(1)}, u32[]{:S(2)}) copy-start(f32[2,64,64]{1,2,0:T(8,128)S(1)} %copy.326) | copy-start | bytes 98308
  143.4 24.5 %copy-start.99 = (f32[2,64]{1,0:T(2,128)}, f32[2,64]{1,0:T(2,128)S(1)}, u32[]{:S(2)}) copy-start(f32[2,64]{1,0:T(2,128)S(1)} %get-tuple-element.82) | copy-start | bytes 1540
  143.5 24.5 %copy-start.101 = (f32[2,64]{1,0:T(2,128)}, f32[2,64]{1,0:T(2,128)S(1)}, u32[]{:S(2)}) copy-start(f32[2,64]{1,0:T(2,128)S(1)} %get-tuple-element.81) | copy-start | bytes 1540
  143.6 24.4 %copy-start.105 = (f32[2]{0:T(128)}, f32[2]{0:T(128)S(1)}, u32[]{:S(2)}) copy-start(f32[2]{0:T(128)S(1)} %reduce_max.55) | copy-start | bytes 28
  143.7 24.2 %copy-start.107 = (f32[2]{0:T(128)}, f32[2]{0:T(128)S(1)}, u32[]{:S(2)}) copy-start(f32[2]{0:T(128)S(1)} %reduce_max.56) | copy-start | bytes 28
  144.2 23.7 %copy-start.114 = (f32[2]{0:T(128)}, f32[2]{0:T(128)S(1)}, u32[]{:S(2)}) copy-start(f32[2]{0:T(128)S(1)} %get-tuple-element.96) | copy-start | bytes 28
  146.0 22.8 %copy-start.33 = (f32[1,2,16,4,768]{4,3,1,0,2:T(4,128)S(1)}, f32[1,2,16,4,768]{4,3,1,0,2:T(4,128)}, u32[]{:S(2)}) copy-start(f32[1,2,16,4,768]{4,3,1,0,2:T(4,128)} %get-tuple-element.106) | copy-start | bytes 1179652
  149.5 17.4 %copy-start.50 = (f32[2,64,64]{2,1,0:T(8,128)}, f32[2,64,64]{2,1,0:T(8,128)S(1)}, u32[]{:S(2)}) copy-start(f32[2,64,64]{2,1,0:T(8,128)S(1)} %convolution_subtract_fusion.6) | copy-start | bytes 98308
  149.7 22.0 %copy-start.43 = (f32[2,64,64]{2,1,0:T(8,128)}, f32[2,64,64]{2,1,0:T(8,128)S(1)}, u32[]{:S(2)}) copy-start(f32[2,64,64]{2,1,0:T(8,128)S(1)} %convolution_multiply_fusion.9) | copy-start | bytes 98308
  150.1 21.7 %copy-start.26 = (f32[2,64,64]{2,1,0:T(8,128)}, f32[2,64,64]{2,1,0:T(8,128)S(1)}, u32[]{:S(2)}) copy-start(f32[2,64,64]{2,1,0:T(8,128)S(1)} %fusion.134) | copy-start | bytes 98308
  150.5 16.5 %copy-start.52 = (f32[2,64,64]{2,1,0:T(8,128)}, f32[2,64,64]{2,1,0:T(8,128)S(1)}, u32[]{:S(2)}) copy-start(f32[2,64,64]{2,1,0:T(8,128)S(1)} %convolution_subtract_fusion.4) | copy-start | bytes 98308
  150.7 21.0 %copy-start.38 = (f32[2,64,64]{2,1,0:T(8,128)}, f32[2,64,64]{2,1,0:T(8,128)S(1)}, u32[]{:S(2)}) copy-start(f32[2,64,64]{2,1,0:T(8,128)S(1)} %convolution_multiply_fusion.8) | copy-start | bytes 98308
  151.0 20.7 %copy-start.27 = (f32[2,64,64]{2,1,0:T(8,128)}, f32[2,64,64]{2,1,0:T(8,128)S(1)}, u32[]{:S(2)}) copy-start(f32[2,64,64]{2,1,0:T(8,128)S(1)} %fusion.133) | copy-start | bytes 98308
  152.1 14.9 %copy-start.54 = (f32[2,64,64]{2,1,0:T(8,128)}, f32[2,64,64]{2,1,0:T(8,128)S(1)}, u32[]{:S(2)}) copy-start(f32[2,64,64]{2,1,0:T(8,128)S(1)} %convolution_subtract_fusion.2) | copy-start | bytes 98308
  152.3 14.7 %copy-start.55 = (f32[2,64,64]{2,1,0:T(8,128)}, f32[2,64,64]{2,1,0:T(8,128)S(1)}, u32[]{:S(2)}) copy-start(f32[2,64,64]{2,1,0:T(8,128)S(1)} %convolution_multiply_fusion.7) | copy-start | bytes 98308
  168.8 7.2 %copy-start.34 = (bf16[12,2,64,64]{2,3,1,0:T(8,128)(2,1)}, bf16[12,2,64,64]{2,3,1,0:T(8,128)(2,1)S(1)}, u32[]{:S(2)}) copy-start(bf16[12,2,64,64]{2,3,1,0:T(8,128)(2,1)S(1)} %copy.314) | copy-start | bytes 589828
  176.0 46.9 %copy-start.77 = (f32[2,12,128]{2,1,0:T(8,128)}, f32[2,12,128]{2,1,0:T(8,128)S(1)}, u32[]{:S(2)}) copy-start(f32[2,12,128]{2,1,0:T(8,128)S(1)} %get-tuple-element.144) | copy-start | bytes 36868
  181.8 9.4 %copy-start.17 = (bf16[2,128,12,64]{1,3,2,0:T(8,128)(2,1)}, bf16[2,128,12,64]{1,3,2,0:T(8,128)(2,1)S(1)}, u32[]{:S(2)}) copy-start(bf16[2,128,12,64]{1,3,2,0:T(8,128)(2,1)S(1)} %fusion.21) | copy-start | bytes 1179652
  184.6 6.6 %copy-start.91 = (f32[2,128]{1,0:T(2,128)}, f32[2,128]{1,0:T(2,128)S(1)}, u32[]{:S(2)}) copy-start(f32[2,128]{1,0:T(2,128)S(1)} %fusion.128) | copy-start | bytes 3076
  191.3 8.6 %copy-start.22 = (f32[2,128,3072]{2,1,0:T(8,128)}, f32[2,128,3072]{2,1,0:T(8,128)S(1)}, u32[]{:S(2)}) copy-start(f32[2,128,3072]{2,1,0:T(8,128)S(1)} %get-tuple-element.148) | copy-start | bytes 9437188
  191.3 8.6 %copy-start.81 = (f32[1,32,24]{2,1,0:T(8,128)S(1)}, f32[1,32,24]{2,1,0:T(8,128)}, u32[]{:S(2)}) copy-start(f32[1,32,24]{2,1,0:T(8,128)} %get-tuple-element.114) | copy-start | bytes 9220
  209.0 9.7 %slice-start = ((s8[4718592]{0:T(1024)(128)(4,1)}), s8[4194304]{0:T(1024)(128)(4,1)S(1)}, s32[]{:S(2)}) async-start(s8[4718592]{0:T(1024)(128)(4,1)} %bitcast.533), calls=%async_computation | async-start | bytes 8388608
  211.6 7.1 %copy-start.30 = (bf16[2,128,768]{2,1,0:T(8,128)(2,1)}, bf16[2,128,768]{2,1,0:T(8,128)(2,1)S(1)}, u32[]{:S(2)}) copy-start(bf16[2,128,768]{2,1,0:T(8,128)(2,1)S(1)} %get-tuple-element.86) | copy-start | bytes 1179652
  211.6 7.1 %copy-start.92 = (f32[2,128]{1,0:T(2,128)S(1)}, f32[2,128]{1,0:T(2,128)}, u32[]{:S(2)}) copy-start(f32[2,128]{1,0:T(2,128)} %copy-done.91) | copy-start | bytes 3076
  211.6 7.1 %copy-start.96 = (f32[2,128]{1,0:T(2,128)S(1)}, f32[2,128]{1,0:T(2,128)}, u32[]{:S(2)}) copy-start(f32[2,128]{1,0:T(2,128)} %copy-done.95) | copy-start | bytes 3076
  211.6 7.1 %copy-start.109 = (f32[2,128]{1,0:T(2,128)S(1)}, f32[2,128]{1,0:T(2,128)}, u32[]{:S(2)}) copy-start(f32[2,128]{1,0:T(2,128)} %negate_multiply_fusion.2) | copy-start | bytes 3076
  211.6 7.1 %slice-start.1 = ((s8[4718592]{0:T(1024)(128)(4,1)}), s8[524288]{0:T(1024)(128)(4,1)S(1)}, s32[]{:S(2)}) async-start(s8[4718592]{0:T(1024)(128)(4,1)} %bitcast.533), calls=%async_computation.1 | async-start | bytes 1048576
  272.0 13.8 %copy-start.90 = (f32[2,12,64]{2,1,0:T(8,128)}, f32[2,12,64]{2,1,0:T(8,128)S(1)}, u32[]{:S(2)}) copy-start(f32[2,12,64]{2,1,0:T(8,128)S(1)} %div.189) | copy-start | bytes 18436
  277.9 14.8 %copy-start.44 = (f32[2,64,64]{2,1,0:T(8,128)S(1)}, f32[2,64,64]{2,1,0:T(8,128)}, u32[]{:S(2)}) copy-start(f32[2,64,64]{2,1,0:T(8,128)} %copy-done.43) | copy-start | bytes 98308
  277.9 15.1 %copy-start.53 = (f32[2,64,64]{2,1,0:T(8,128)S(1)}, f32[2,64,64]{2,1,0:T(8,128)}, u32[]{:S(2)}) copy-start(f32[2,64,64]{2,1,0:T(8,128)} %copy-done.52) | copy-start | bytes 98308
  277.9 15.5 %copy-start.42 = (f32[2,64,64]{2,1,0:T(8,128)S(1)}, f32[2,64,64]{2,1,0:T(8,128)}, u32[]{:S(2)}) copy-start(f32[2,64,64]{2,1,0:T(8,128)} %copy-done.41) | copy-start | bytes 98308
  277.9 16.1 %copy-start.66 = (f32[2,64,64]{2,1,0:T(8,128)S(1)}, f32[2,64,64]{2,1,0:T(8,128)}, u32[]{:S(2)}) copy-start(f32[2,64,64]{2,1,0:T(8,128)} %copy-done.65) | copy-start | bytes 98308
  277.9 17.2 %copy-start.51 = (f32[2,64,64]{2,1,0:T(8,128)S(1)}, f32[2,64,64]{2,1,0:T(8,128)}, u32[]{:S(2)}) copy-start(f32[2,64,64]{2,1,0:T(8,128)} %copy-done.50) | copy-start | bytes 98308
  277.9 17.7 %copy-start.40 = (f32[2,64,64]{2,1,0:T(8,128)S(1)}, f32[2,64,64]{2,1,0:T(8,128)}, u32[]{:S(2)}) copy-start(f32[2,64,64]{2,1,0:T(8,128)} %copy-done.39) | copy-start | bytes 98308
  277.9 18.3 %copy-start.64 = (f32[2,64,64]{2,1,0:T(8,128)S(1)}, f32[2,64,64]{2,1,0:T(8,128)}, u32[]{:S(2)}) copy-start(f32[2,64,64]{2,1,0:T(8,128)} %copy-done.63) | copy-start | bytes 98308
  282.4 14.8 %copy-start.49 = (f32[2,64,64]{2,1,0:T(8,128)S(1)}, f32[2,64,64]{2,1,0:T(8,128)}, u32[]{:S(2)}) copy-start(f32[2,64,64]{2,1,0:T(8,128)} %copy-done.48) | copy-start | bytes 98308
  284.6 13.0 %copy-start.60 = (f32[2,64,64]{2,1,0:T(8,128)S(1)}, f32[2,64,64]{2,1,0:T(8,128)}, u32[]{:S(2)}) copy-start(f32[2,64,64]{2,1,0:T(8,128)} %copy-done.59) | copy-start | bytes 98308
  286.8 11.4 %copy-start.62 = (f32[2,64,64]{2,1,0:T(8,128)S(1)}, f32[2,64,64]{2,1,0:T(8,128)}, u32[]{:S(2)}) copy-start(f32[2,64,64]{2,1,0:T(8,128)} %copy-done.61) | copy-start | bytes 98308
  290.4 8.9 %copy-start.47 = (f32[2,64,64]{2,1,0:T(8,128)S(1)}, f32[2,64,64]{2,1,0:T(8,128)}, u32[]{:S(2)}) copy-start(f32[2,64,64]{2,1,0:T(8,128)} %copy-done.46) | copy-start | bytes 98308
  292.7 7.0 %copy-start.115 = (f32[2]{0:T(128)S(1)}, f32[2]{0:T(128)}, u32[]{:S(2)}) copy-start(f32[2]{0:T(128)} %copy-done.114) | copy-start | bytes 28
  293.2 7.2 %copy-start.58 = (f32[2,64,64]{2,1,0:T(8,128)S(1)}, f32[2,64,64]{2,1,0:T(8,128)}, u32[]{:S(2)}) copy-start(f32[2,64,64]{2,1,0:T(8,128)} %copy-done.57) | copy-start | bytes 98308
  294.2 6.9 %copy-start.71 = (f32[2,64,64]{2,1,0:T(8,128)S(1)}, f32[2,64,64]{2,1,0:T(8,128)}, u32[]{:S(2)}) copy-start(f32[2,64,64]{2,1,0:T(8,128)} %copy-done.70) | copy-start | bytes 98308
  294.3 7.2 %copy-start.116 = (f32[2]{0:T(128)S(1)}, f32[2]{0:T(128)}, u32[]{:S(2)}) copy-start(f32[2]{0:T(128)} %get-tuple-element.95) | copy-start | bytes 28
  294.8 6.9 %copy-start.102 = (f32[2,64]{1,0:T(2,128)S(1)}, f32[2,64]{1,0:T(2,128)}, u32[]{:S(2)}) copy-start(f32[2,64]{1,0:T(2,128)} %copy-done.101) | copy-start | bytes 1540
  294.8 6.9 %copy-start.108 = (f32[2]{0:T(128)S(1)}, f32[2]{0:T(128)}, u32[]{:S(2)}) copy-start(f32[2]{0:T(128)} %copy-done.107) | copy-start | bytes 28
  294.8 7.1 %copy-start.100 = (f32[2,64]{1,0:T(2,128)S(1)}, f32[2,64]{1,0:T(2,128)}, u32[]{:S(2)}) copy-start(f32[2,64]{1,0:T(2,128)} %copy-done.99) | copy-start | bytes 1540
  294.8 7.1 %copy-start.106 = (f32[2]{0:T(128)S(1)}, f32[2]{0:T(128)}, u32[]{:S(2)}) copy-start(f32[2]{0:T(128)} %copy-done.105) | copy-start | bytes 28
  295.6 7.7 %copy-start.75 = (f32[64,2,64]{2,1,0:T(2,128)S(1)}, f32[64,2,64]{2,1,0:T(2,128)}, u32[]{:S(2)}) copy-start(f32[64,2,64]{2,1,0:T(2,128)} %copy-done.74) | copy-start | bytes 98308
  302.6 9.1 %copy-start.117 = (f32[2,64,64]{1,2,0:T(8,128)}, f32[2,64,64]{1,2,0:T(8,128)S(1)}, u32[]{:S(2)}) copy-start(f32[2,64,64]{1,2,0:T(8,128)S(1)} %get-tuple-element.157) | copy-start | bytes 98308
  304.6 11.5 %copy-start.73 = (f32[64,2,64]{2,1,0:T(2,128)S(1)}, f32[64,2,64]{2,1,0:T(2,128)}, u32[]{:S(2)}) copy-start(f32[64,2,64]{2,1,0:T(2,128)} %copy-done.72) | copy-start | bytes 98308
  304.6 11.5 %copy-start.113 = (f32[2,64]{1,0:T(2,128)S(1)}, f32[2,64]{1,0:T(2,128)}, u32[]{:S(2)}) copy-start(f32[2,64]{1,0:T(2,128)} %copy-done.112) | copy-start | bytes 1540
  307.5 9.8 %copy-start.78 = (f32[2,12,128]{2,1,0:T(8,128)S(1)}, f32[2,12,128]{2,1,0:T(8,128)}, u32[]{:S(2)}) copy-start(f32[2,12,128]{2,1,0:T(8,128)} %copy-done.77) | copy-start | bytes 36868
  307.5 9.8 %copy-start.13 = (f32[2,12,128,64]{2,3,1,0:T(8,128)S(1)}, f32[2,12,128,64]{2,3,1,0:T(8,128)}, u32[]{:S(2)}) copy-start(f32[2,12,128,64]{2,3,1,0:T(8,128)} %copy-done.11) | copy-start | bytes 2359300
  357.1 7.1 %copy-start.89 = (f32[768]{0:T(1024)S(1)}, f32[768]{0:T(1024)}, u32[]{:S(2)}) copy-start(f32[768]{0:T(1024)} %get-tuple-element.87) | copy-start | bytes 9220
  357.1 7.2 %copy-start.88 = (f32[768]{0:T(1024)S(1)}, f32[768]{0:T(1024)}, u32[]{:S(2)}) copy-start(f32[768]{0:T(1024)} %get-tuple-element.85) | copy-start | bytes 9220
  357.1 7.3 %copy-start.111 = (f32[768]{0:T(1024)S(1)}, f32[768]{0:T(1024)}, u32[]{:S(2)}) copy-start(f32[768]{0:T(1024)} %get-tuple-element.73) | copy-start | bytes 9220
  357.1 7.4 %copy-start.110 = (f32[768]{0:T(1024)S(1)}, f32[768]{0:T(1024)}, u32[]{:S(2)}) copy-start(f32[768]{0:T(1024)} %get-tuple-element.79) | copy-start | bytes 9220
  357.1 7.5 %copy-start.87 = (f32[768]{0:T(1024)S(1)}, f32[768]{0:T(1024)}, u32[]{:S(2)}) copy-start(f32[768]{0:T(1024)} %get-tuple-element.75) | copy-start | bytes 9220
  357.1 7.6 %copy-start.86 = (f32[768]{0:T(1024)S(1)}, f32[768]{0:T(1024)}, u32[]{:S(2)}) copy-start(f32[768]{0:T(1024)} %get-tuple-element.80) | copy-start | bytes 9220
  357.1 8.4 %copy-start.94 = (f32[3072]{0:T(1024)S(1)}, f32[3072]{0:T(1024)}, u32[]{:S(2)}) copy-start(f32[3072]{0:T(1024)} %get-tuple-element.163) | copy-start | bytes 36868
  380.8 7.0 %copy-start.5 = (f32[2,64,12,64]{1,3,2,0:T(8,128)S(1)}, f32[2,64,12,64]{1,3,2,0:T(8,128)}, u32[]{:S(2)}) copy-start(f32[2,64,12,64]{1,3,2,0:T(8,128)} %copy-done.4) | copy-start | bytes 1179652
  486.8 7.0 %copy-start.1 = (bf16[12,33]{1,0:T(8,128)(2,1)S(1)}, bf16[12,33]{1,0:T(8,128)(2,1)}, u32[]{:S(2)}) copy-start(bf16[12,33]{1,0:T(8,128)(2,1)} %param.34) | copy-start | bytes 2380
  (56 other events, 175.1 us)
